TPU v7x, 32 devices: a whole 2x2x4 slice. The times are simulated.
32 devices in a mesh: dp: 8 (over z, x), tensor: 4 (over y, core).
Axes of the slice: x: 2, y: 2, z: 4, core: 2. Of those that a mesh axis runs over, the one named last changes fastest.
Arguments:
- tokens: bfloat16 [16, 128, 2048], P('dp'), may hold values from -6 to 6
- cotangent: bfloat16 [16, 128, 2048], P('dp'), may hold values from -6 to 6
- routes: int32 [16, 128, 4], P('dp'), may hold values from 0 to 5, as said below
- gates: bfloat16 [16, 128, 4], P('dp'), may hold values from 0.099609375 to 0.5
- lengths: int32 [16], P('dp'), may hold values from 64 to 128, as said below
- deal: int32 [16], replicated, may hold values from 0 to 15, as said below
- norm1_gain: float32 [2048], P('dp'), may hold values from 0.1 to 1.9
- q_weight: float32 [2048, 2048], P('dp', 'tensor'), may hold values from -0.125 to 0.125
- q_bias: float32 [16, 128], P('tensor', 'dp'), may hold values from -3 to 3
- k_weight: float32 [2048, 2048], P('dp', 'tensor'), may hold values from -0.125 to 0.125
- v_weight: float32 [2048, 2048], P('dp', 'tensor'), may hold values from -0.125 to 0.125
- v_bias: float32 [16, 128], P('tensor', 'dp'), may hold values from -3 to 3
- o_weight: float32 [2048, 2048], P('tensor', 'dp'), may hold values from -0.75 to 0.75
- norm2_gain: float32 [2048], P('dp'), may hold values from 0.1 to 1.9
- expert_gate: float32 [6, 2048, 1408], P(None, 'dp', 'tensor'), may hold values from -0.125 to 0.125
- expert_up: float32 [6, 2048, 1408], P(None, 'dp', 'tensor'), may hold values from -0.125 to 0.125
- expert_down: float32 [6, 1408, 2048], P(None, 'tensor', 'dp'), may hold values from -0.21875 to 0.21875
- shared_gate: float32 [2048, 5632], P('dp', 'tensor'), may hold values from -0.125 to 0.125
- shared_up: float32 [2048, 5632], P('dp', 'tensor'), may hold values from -0.125 to 0.125
- shared_down: float32 [5632, 2048], P('tensor', 'dp'), may hold values from -0.109375 to 0.109375
- shared_switch: float32 [2048], P('dp'), may hold values from -0.125 to 0.125
Outputs:
- output: float32 [16, 128, 2048], P('dp', None, 'tensor')
- tokens_grad: float32 [16, 128, 2048], P('dp', None, 'tensor')
- norm1_gain_grad: float32 [2048], P('dp')
- q_weight_grad: float32 [2048, 2048], P('dp', 'tensor')
- q_bias_grad: float32 [16, 128], P('tensor', 'dp')
- k_weight_grad: float32 [2048, 2048], P('dp', 'tensor')
- v_weight_grad: float32 [2048, 2048], P('dp', 'tensor')
- v_bias_grad: float32 [16, 128], P('tensor', 'dp')
- o_weight_grad: float32 [2048, 2048], P('tensor', 'dp')
- norm2_gain_grad: float32 [2048], P('dp')
- expert_gate_grad: float32 [6, 2048, 1408], P(None, 'dp', 'tensor')
- expert_up_grad: float32 [6, 2048, 1408], P(None, 'dp', 'tensor')
- expert_down_grad: float32 [6, 1408, 2048], P(None, 'tensor', 'dp')
- shared_gate_grad: float32 [2048, 5632], P('dp', 'tensor')
- shared_up_grad: float32 [2048, 5632], P('dp', 'tensor')
- shared_down_grad: float32 [5632, 2048], P('tensor', 'dp')
- shared_switch_grad: float32 [2048], P('dp')
Inputs may be any that keep to these rules, and one draw needn't show every extreme that they name: Sequences 2i and 2i+1 are given on dp index i. The two sequences dealt to one dp index have lengths adding up to exactly 192. `deal`: dealt slot 2i holds sequence 2i; the odd sequences move by one common rotation of the dp indices: slot 2i+1 holds sequence 2((i - r) mod the number of dp indices) + 1, for one r of the draw. `routes`: each row names 4 different experts. Among the 192 real tokens dealt to one dp index, every expert is named by exactly 128 tokens. Rows past a sequence's length hold valid ids too.
All inputs are finite; a program needn't handle non-finite values.
Results may differ from a plain program's by a relative error of at most 0.013.
The roundings to bfloat16 on the way count: a program that leaves them out, or rounds other values in their place, can miss the bound.
Values may be sent and summed in bfloat16 or wider, within the bound.
A program may use at most 256 MiB of HBM per device.

v0:
```python
from functools import partial

import jax
import jax.numpy as jnp
from jax import lax
from jax.sharding import PartitionSpec as P

D = 2048
HEAD_DIM = 128
EXPERTS = 6
TOP = 4
LMAX = 128
SPAN = 192
CAPACITY = 128


EPSILON = 1e-06
NEGATIVE = -1e30


def as_sent(value):

    def short(part):
        return part.astype(jnp.bfloat16) if part.dtype == jnp.float32 else part

    return jax.tree.map(short, value)


def shifted(value, axis, steps):
    count = lax.axis_size(axis)
    pairs = [(source, (source + steps) % count) for source in range(count)]
    return lax.ppermute(value, axis, pairs)


def normalize(values, gain):
    return values * lax.rsqrt(jnp.mean(values * values, axis=-1, keepdims=True) + EPSILON) * gain


def silu_slope(values):
    logistic = jax.nn.sigmoid(values)
    return logistic * (1.0 + values * (1.0 - logistic))


def masked_scores(query_heads, key_heads, allowed):
    scores = jnp.einsum(
        "qhd,khd->hqk", query_heads, key_heads, preferred_element_type=jnp.float32
    ) * HEAD_DIM ** (-0.5)
    return jnp.where(allowed[None], scores, NEGATIVE)


def per_device(
    tokens,
    cotangent,
    routes,
    gates,
    lengths,
    deal,
    norm1_gain,
    q_weight,
    q_bias,
    k_weight,
    v_weight,
    v_bias,
    o_weight,
    norm2_gain,
    expert_gate,
    expert_up,
    expert_down,
    shared_gate,
    shared_up,
    shared_down,
    shared_switch,
):
    devices = lax.axis_size("dp")
    levels = devices.bit_length() - 1
    offset = (devices - (deal[1] - 1) // 2) % devices
    moving = (tokens[1], cotangent[1], routes[1], gates[1], lengths[1:2])
    for level in range(levels):
        arrived = jax.tree.map(
            lambda part, own: part.astype(own.dtype),
            shifted(as_sent(moving), "dp", 1 << level),
            moving,
        )
        taken = offset // (1 << level) % 2 == 1
        moving = jax.tree.map(partial(jnp.where, taken), arrived, moving)
    first_len = lengths[0]

    def pack_rows(front_part, back_part):
        buffer = jnp.zeros((SPAN + LMAX,) + front_part.shape[1:], front_part.dtype)
        buffer = lax.dynamic_update_slice_in_dim(buffer, front_part, 0, 0)
        buffer = lax.dynamic_update_slice_in_dim(buffer, back_part, first_len, 0)
        return buffer[:SPAN]

    packed_tokens = pack_rows(tokens[0], moving[0])
    packed_cot = pack_rows(cotangent[0], moving[1])
    packed_routes = pack_rows(routes[0], moving[2])
    packed_gates = pack_rows(gates[0], moving[3]).astype(jnp.float32)
    positions = jnp.arange(SPAN)
    second_doc = positions >= first_len
    allowed = (positions[None, :] <= positions[:, None]) & (
        second_doc[None, :] == second_doc[:, None]
    )
    gain_one, weight_q, bias_q, weight_k, weight_v, bias_v, weight_o = (
        lax.all_gather(norm1_gain.astype(jnp.bfloat16), "dp", axis=0, tiled=True),
        lax.all_gather(q_weight.astype(jnp.bfloat16), "dp", axis=0, tiled=True),
        lax.all_gather(q_bias.astype(jnp.bfloat16), "dp", axis=1, tiled=True),
        lax.all_gather(k_weight.astype(jnp.bfloat16), "dp", axis=0, tiled=True),
        lax.all_gather(v_weight.astype(jnp.bfloat16), "dp", axis=0, tiled=True),
        lax.all_gather(v_bias.astype(jnp.bfloat16), "dp", axis=1, tiled=True),
        lax.all_gather(o_weight.astype(jnp.bfloat16), "dp", axis=1, tiled=True),
    )
    (
        gain_two,
        gate_experts,
        up_experts,
        down_experts,
        gate_shared,
        up_shared,
        down_shared,
        switch_vector,
    ) = (
        lax.all_gather(norm2_gain.astype(jnp.bfloat16), "dp", axis=0, tiled=True),
        lax.all_gather(expert_gate.astype(jnp.bfloat16), "dp", axis=1, tiled=True),
        lax.all_gather(expert_up.astype(jnp.bfloat16), "dp", axis=1, tiled=True),
        lax.all_gather(expert_down.astype(jnp.bfloat16), "dp", axis=2, tiled=True),
        lax.all_gather(shared_gate.astype(jnp.bfloat16), "dp", axis=0, tiled=True),
        lax.all_gather(shared_up.astype(jnp.bfloat16), "dp", axis=0, tiled=True),
        lax.all_gather(shared_down.astype(jnp.bfloat16), "dp", axis=1, tiled=True),
        lax.all_gather(shared_switch.astype(jnp.bfloat16), "dp", axis=0, tiled=True),
    )
    inputs = packed_tokens.astype(jnp.float32)
    normed_one = normalize(inputs, gain_one.astype(jnp.float32)).astype(jnp.bfloat16)
    queries = (
        jnp.dot(normed_one, weight_q, preferred_element_type=jnp.float32) + bias_q.reshape(-1)
    ).astype(jnp.bfloat16)
    key_rows = jnp.dot(normed_one, weight_k, preferred_element_type=jnp.float32).astype(
        jnp.bfloat16
    )
    value_rows = (
        jnp.dot(normed_one, weight_v, preferred_element_type=jnp.float32) + bias_v.reshape(-1)
    ).astype(jnp.bfloat16)
    local_heads = queries.shape[1] // HEAD_DIM
    head_shape = (SPAN, local_heads, HEAD_DIM)
    query_heads = queries.reshape(head_shape)
    key_heads = key_rows.reshape(head_shape)
    value_heads = value_rows.reshape(head_shape)
    scores = masked_scores(query_heads, key_heads, allowed)
    top_score = jnp.max(scores, axis=-1, keepdims=True)
    log_total = top_score + jnp.log(jnp.sum(jnp.exp(scores - top_score), axis=-1, keepdims=True))
    attn_probs = jnp.exp(scores - log_total)
    attended = (
        jnp.einsum(
            "hqk,khd->qhd",
            attn_probs.astype(jnp.bfloat16),
            value_heads,
            preferred_element_type=jnp.float32,
        )
        .reshape(SPAN, -1)
        .astype(jnp.bfloat16)
    )
    attn_part = jnp.dot(attended, weight_o, preferred_element_type=jnp.float32)
    middle = inputs + lax.psum(attn_part, "tensor")
    normed_two = normalize(middle, gain_two.astype(jnp.float32)).astype(jnp.bfloat16)
    flat_routes = packed_routes.reshape(-1)
    onehot = (flat_routes[:, None] == jnp.arange(EXPERTS)[None, :]).astype(jnp.int32)
    earlier = jnp.cumsum(onehot, axis=0) - onehot
    place_in = jnp.sum(earlier * onehot, axis=1)
    slot_of = flat_routes * CAPACITY + place_in
    token_of_slot = (
        jnp.zeros((EXPERTS * CAPACITY,), jnp.int32)
        .at[slot_of]
        .set(jnp.arange(SPAN * TOP, dtype=jnp.int32) // TOP)
    )
    weight_of_slot = (
        jnp.zeros((EXPERTS * CAPACITY,), jnp.float32).at[slot_of].set(packed_gates.reshape(-1))
    )
    slot_grid = slot_of.reshape(SPAN, TOP)
    expert_in = normed_two[token_of_slot].reshape(EXPERTS, CAPACITY, -1)
    gate_act = jnp.einsum(
        "ecd,edf->ecf", expert_in, gate_experts, preferred_element_type=jnp.float32
    )
    up_act = jnp.einsum("ecd,edf->ecf", expert_in, up_experts, preferred_element_type=jnp.float32)
    inner_act = (jax.nn.silu(gate_act) * up_act).astype(jnp.bfloat16)
    expert_out = jnp.einsum(
        "ecf,efd->ecd", inner_act, down_experts, preferred_element_type=jnp.float32
    ).reshape(EXPERTS * CAPACITY, -1)
    expert_mix = jnp.zeros_like(middle)
    for rank_slot in range(TOP):
        expert_mix = (
            expert_mix + packed_gates[:, rank_slot, None] * expert_out[slot_grid[:, rank_slot]]
        )
    shared_act = jnp.dot(normed_two, gate_shared, preferred_element_type=jnp.float32)
    shared_lift = jnp.dot(normed_two, up_shared, preferred_element_type=jnp.float32)
    shared_inner = (jax.nn.silu(shared_act) * shared_lift).astype(jnp.bfloat16)
    shared_out = jnp.dot(shared_inner, down_shared, preferred_element_type=jnp.float32)
    switch_gate = jax.nn.sigmoid(
        jnp.dot(normed_two, switch_vector, preferred_element_type=jnp.float32)
    )
    ffn_part = expert_mix + switch_gate[:, None] * shared_out
    result = middle + lax.psum(ffn_part.astype(jnp.bfloat16), "tensor").astype(jnp.float32)
    grad_out = packed_cot.astype(jnp.float32)
    (
        gain_two,
        gate_experts,
        up_experts,
        down_experts,
        gate_shared,
        up_shared,
        down_shared,
        switch_vector,
    ) = (
        lax.all_gather(norm2_gain.astype(jnp.bfloat16), "dp", axis=0, tiled=True),
        lax.all_gather(expert_gate.astype(jnp.bfloat16), "dp", axis=1, tiled=True),
        lax.all_gather(expert_up.astype(jnp.bfloat16), "dp", axis=1, tiled=True),
        lax.all_gather(expert_down.astype(jnp.bfloat16), "dp", axis=2, tiled=True),
        lax.all_gather(shared_gate.astype(jnp.bfloat16), "dp", axis=0, tiled=True),
        lax.all_gather(shared_up.astype(jnp.bfloat16), "dp", axis=0, tiled=True),
        lax.all_gather(shared_down.astype(jnp.bfloat16), "dp", axis=1, tiled=True),
        lax.all_gather(shared_switch.astype(jnp.bfloat16), "dp", axis=0, tiled=True),
    )
    grad_shared = (switch_gate[:, None] * grad_out).astype(jnp.bfloat16)
    grad_down_shared = jnp.dot(shared_inner.T, grad_shared, preferred_element_type=jnp.float32)
    grad_shared_inner = jnp.dot(grad_shared, down_shared.T, preferred_element_type=jnp.float32)
    grad_logit = jnp.sum(grad_out * shared_out, axis=1) * switch_gate * (1.0 - switch_gate)
    grad_shared_act = (grad_shared_inner * shared_lift * silu_slope(shared_act)).astype(
        jnp.bfloat16
    )
    grad_shared_lift = (grad_shared_inner * jax.nn.silu(shared_act)).astype(jnp.bfloat16)
    grad_gate_shared = jnp.dot(normed_two.T, grad_shared_act, preferred_element_type=jnp.float32)
    grad_up_shared = jnp.dot(normed_two.T, grad_shared_lift, preferred_element_type=jnp.float32)
    grad_switch = jnp.dot(grad_logit, normed_two, preferred_element_type=jnp.float32)
    back_two = (
        jnp.dot(grad_shared_act, gate_shared.T, preferred_element_type=jnp.float32)
        + jnp.dot(grad_shared_lift, up_shared.T, preferred_element_type=jnp.float32)
        + grad_logit[:, None] * switch_vector.astype(jnp.float32)[None, :]
    )
    grad_slot = (
        (grad_out[token_of_slot] * weight_of_slot[:, None])
        .astype(jnp.bfloat16)
        .reshape(EXPERTS, CAPACITY, -1)
    )
    grad_down_experts = jnp.einsum(
        "ecf,ecd->efd", inner_act, grad_slot, preferred_element_type=jnp.float32
    )
    grad_inner = jnp.einsum(
        "ecd,efd->ecf", grad_slot, down_experts, preferred_element_type=jnp.float32
    )
    grad_gate_act = (grad_inner * up_act * silu_slope(gate_act)).astype(jnp.bfloat16)
    grad_up_act = (grad_inner * jax.nn.silu(gate_act)).astype(jnp.bfloat16)
    grad_gate_experts = jnp.einsum(
        "ecd,ecf->edf", expert_in, grad_gate_act, preferred_element_type=jnp.float32
    )
    grad_up_experts = jnp.einsum(
        "ecd,ecf->edf", expert_in, grad_up_act, preferred_element_type=jnp.float32
    )
    grad_expert_in = (
        jnp.einsum("ecf,edf->ecd", grad_gate_act, gate_experts, preferred_element_type=jnp.float32)
        + jnp.einsum("ecf,edf->ecd", grad_up_act, up_experts, preferred_element_type=jnp.float32)
    ).reshape(EXPERTS * CAPACITY, -1)
    for rank_slot in range(TOP):
        back_two = back_two + grad_expert_in[slot_grid[:, rank_slot]]
    back_two, grad_switch = lax.psum((back_two, grad_switch), "tensor")
    unused_two, norm_two_back = jax.vjp(normalize, middle, gain_two.astype(jnp.float32))
    grad_middle_norm, grad_gain_two = norm_two_back(back_two)
    grad_middle = grad_out + grad_middle_norm
    gain_one, weight_q, bias_q, weight_k, weight_v, bias_v, weight_o = (
        lax.all_gather(norm1_gain.astype(jnp.bfloat16), "dp", axis=0, tiled=True),
        lax.all_gather(q_weight.astype(jnp.bfloat16), "dp", axis=0, tiled=True),
        lax.all_gather(q_bias.astype(jnp.bfloat16), "dp", axis=1, tiled=True),
        lax.all_gather(k_weight.astype(jnp.bfloat16), "dp", axis=0, tiled=True),
        lax.all_gather(v_weight.astype(jnp.bfloat16), "dp", axis=0, tiled=True),
        lax.all_gather(v_bias.astype(jnp.bfloat16), "dp", axis=1, tiled=True),
        lax.all_gather(o_weight.astype(jnp.bfloat16), "dp", axis=1, tiled=True),
    )
    grad_attn = grad_middle.astype(jnp.bfloat16)
    grad_weight_o = jnp.dot(attended.T, grad_attn, preferred_element_type=jnp.float32)
    grad_attended = (
        jnp.dot(grad_attn, weight_o.T, preferred_element_type=jnp.float32)
        .astype(jnp.bfloat16)
        .reshape(head_shape)
    )
    scores_again = masked_scores(query_heads, key_heads, allowed)
    probs_again = jnp.exp(scores_again - log_total)
    grad_value = (
        jnp.einsum(
            "hqk,qhd->khd",
            probs_again.astype(jnp.bfloat16),
            grad_attended,
            preferred_element_type=jnp.float32,
        )
        .astype(jnp.bfloat16)
        .reshape(SPAN, -1)
    )
    grad_probs = jnp.einsum(
        "qhd,khd->hqk", grad_attended, value_heads, preferred_element_type=jnp.float32
    )
    grad_scores = (
        probs_again * (grad_probs - jnp.sum(grad_probs * probs_again, axis=-1, keepdims=True))
    ).astype(jnp.bfloat16)
    score_scale = HEAD_DIM ** (-0.5)
    grad_query = (
        (
            jnp.einsum("hqk,khd->qhd", grad_scores, key_heads, preferred_element_type=jnp.float32)
            * score_scale
        )
        .astype(jnp.bfloat16)
        .reshape(SPAN, -1)
    )
    grad_key = (
        (
            jnp.einsum("hqk,qhd->khd", grad_scores, query_heads, preferred_element_type=jnp.float32)
            * score_scale
        )
        .astype(jnp.bfloat16)
        .reshape(SPAN, -1)
    )
    grad_weight_q = jnp.dot(normed_one.T, grad_query, preferred_element_type=jnp.float32)
    grad_weight_k = jnp.dot(normed_one.T, grad_key, preferred_element_type=jnp.float32)
    grad_weight_v = jnp.dot(normed_one.T, grad_value, preferred_element_type=jnp.float32)
    grad_bias_q = jnp.sum(grad_query.astype(jnp.float32), axis=0).reshape(local_heads, HEAD_DIM)
    grad_bias_v = jnp.sum(grad_value.astype(jnp.float32), axis=0).reshape(local_heads, HEAD_DIM)
    back_one = (
        jnp.dot(grad_query, weight_q.T, preferred_element_type=jnp.float32)
        + jnp.dot(grad_key, weight_k.T, preferred_element_type=jnp.float32)
        + jnp.dot(grad_value, weight_v.T, preferred_element_type=jnp.float32)
    )
    back_one = lax.psum(back_one, "tensor")
    unused_one, norm_one_back = jax.vjp(normalize, inputs, gain_one.astype(jnp.float32))
    grad_input_norm, grad_gain_one = norm_one_back(back_one)
    grad_input = grad_middle + grad_input_norm
    ffn_grads = (
        lax.psum_scatter(grad_gain_two, "dp", scatter_dimension=0, tiled=True),
        lax.psum_scatter(grad_gate_experts, "dp", scatter_dimension=1, tiled=True),
        lax.psum_scatter(grad_up_experts, "dp", scatter_dimension=1, tiled=True),
        lax.psum_scatter(grad_down_experts, "dp", scatter_dimension=2, tiled=True),
        lax.psum_scatter(grad_gate_shared, "dp", scatter_dimension=0, tiled=True),
        lax.psum_scatter(grad_up_shared, "dp", scatter_dimension=0, tiled=True),
        lax.psum_scatter(grad_down_shared, "dp", scatter_dimension=1, tiled=True),
        lax.psum_scatter(grad_switch, "dp", scatter_dimension=0, tiled=True),
    )
    attn_grads = (
        lax.psum_scatter(grad_gain_one, "dp", scatter_dimension=0, tiled=True),
        lax.psum_scatter(grad_weight_q, "dp", scatter_dimension=0, tiled=True),
        lax.psum_scatter(grad_bias_q, "dp", scatter_dimension=1, tiled=True),
        lax.psum_scatter(grad_weight_k, "dp", scatter_dimension=0, tiled=True),
        lax.psum_scatter(grad_weight_v, "dp", scatter_dimension=0, tiled=True),
        lax.psum_scatter(grad_bias_v, "dp", scatter_dimension=1, tiled=True),
        lax.psum_scatter(grad_weight_o, "dp", scatter_dimension=1, tiled=True),
    )
    member = lax.axis_index("tensor")
    column_width = D // lax.axis_size("tensor")
    out_columns = lax.dynamic_slice_in_dim(result, member * column_width, column_width, 1)
    grad_columns = lax.dynamic_slice_in_dim(grad_input, member * column_width, column_width, 1)
    places = jnp.arange(LMAX)

    def unpack(columns):
        extended = jnp.concatenate([columns, jnp.zeros((LMAX, column_width), jnp.float32)], axis=0)
        front_rows = jnp.where((places < first_len)[:, None], extended[:LMAX], 0.0)
        back_rows = lax.dynamic_slice_in_dim(extended, first_len, LMAX, 0)
        back_rows = jnp.where((places < SPAN - first_len)[:, None], back_rows, 0.0)
        return (front_rows, back_rows)

    front_out, back_out = unpack(out_columns)
    front_grad, back_grad = unpack(grad_columns)
    returning = (back_out, back_grad)
    for level in range(levels):
        arrived = shifted(returning, "dp", -(1 << level))
        taken = offset // (1 << level) % 2 == 1
        returning = jax.tree.map(partial(jnp.where, taken), arrived, returning)
    output = jnp.stack([front_out, returning[0]], axis=0)
    tokens_grad = jnp.stack([front_grad, returning[1]], axis=0)
    return (
        output,
        tokens_grad,
        attn_grads[0],
        attn_grads[1],
        attn_grads[2],
        attn_grads[3],
        attn_grads[4],
        attn_grads[5],
        attn_grads[6],
        ffn_grads[0],
        ffn_grads[1],
        ffn_grads[2],
        ffn_grads[3],
        ffn_grads[4],
        ffn_grads[5],
        ffn_grads[6],
        ffn_grads[7],
    )


def solution(mesh):
    placed = (
        P("dp", None, None),
        P("dp", None, None),
        P("dp", None, None),
        P("dp", None, None),
        P("dp"),
        P(),
        P("dp"),
        P("dp", "tensor"),
        P("tensor", "dp"),
        P("dp", "tensor"),
        P("dp", "tensor"),
        P("tensor", "dp"),
        P("tensor", "dp"),
        P("dp"),
        P(None, "dp", "tensor"),
        P(None, "dp", "tensor"),
        P(None, "tensor", "dp"),
        P("dp", "tensor"),
        P("dp", "tensor"),
        P("tensor", "dp"),
        P("dp"),
    )
    return jax.shard_map(
        per_device,
        mesh=mesh,
        in_specs=placed,
        out_specs=(
            P("dp", None, "tensor"),
            P("dp", None, "tensor"),
            P("dp"),
            P("dp", "tensor"),
            P("tensor", "dp"),
            P("dp", "tensor"),
            P("dp", "tensor"),
            P("tensor", "dp"),
            P("tensor", "dp"),
            P("dp"),
            P(None, "dp", "tensor"),
            P(None, "dp", "tensor"),
            P(None, "tensor", "dp"),
            P("dp", "tensor"),
            P("dp", "tensor"),
            P("tensor", "dp"),
            P("dp"),
        ),
        check_vma=False,
    )
```

profile of v0, /device:TPU:0, one launch (start us, length us, event | category | flops | bytes accessed | tf_op | source)
XLA Modules:
  0.0 3145.3 jit_solution(6397644719113213471)
XLA Ops:
  17.2 16.7 collective-permute-done
  34.1 28.2 all-gather.2
  62.5 16.4 all-gather
  79.0 18.4 all-gather.1
  97.9 20.9 collective-permute-done.2
  124.4 13.8 all-gather.18.cloned.1.call-done
  140.9 47.6 %all-gather.16.cloned.1.call-done = bf16[2048,512]{1,0:T(8,128)(2,1)} async-done(((bf16[256,512]{1,0:T(8,128)(2,1)}), bf16[2048,512]{1,0:T(8,128)(2,1)}) %all-gather.16.cloned.1.call-update) | async-done | bytes 2097168 | tf_op jit(solution)/shard_map/all_gather | solution.py:108
  191.2 48.7 %all-gather.22.cloned.1.call-done = bf16[512,2048]{1,0:T(8,128)(2,1)} async-done(((bf16[512,256]{1,0:T(8,128)(2,1)}), bf16[512,2048]{1,0:T(8,128)(2,1)}) %all-gather.22.cloned.1.call-update) | async-done | bytes 2097168 | tf_op jit(solution)/shard_map/all_gather | solution.py:110
  260.9 27.1 all-gather.4
  288.0 21.0 all-gather.3
  335.4 18.9 collective-permute-done.13
  359.4 43.2 %collective-permute-done.14 = bf16[128,2048]{1,0:T(8,128)(2,1)S(1)} collective-permute-done((bf16[128,2048]{1,0:T(8,128)(2,1)S(1)}, bf16[128,2048]{1,0:T(8,128)(2,1)S(1)}, u32[]{:S(2)}, u32[]{:S(2)}) %collective-permute-start.14) | collective-permute-done | bytes 524320 | tf_op jit(solution)/shard_map/ppermute | solution.py:32
  425.5 78.6 %all-gather.32.cloned.1.call-done = bf16[2048,1408]{1,0:T(8,128)(2,1)} async-done(((bf16[256,1408]{1,0:T(8,128)(2,1)}), bf16[2048,1408]{1,0:T(8,128)(2,1)}) %all-gather.32.cloned.1.call-update) | async-done | bytes 5767184 | tf_op jit(solution)/shard_map/all_gather | solution.py:127
  509.5 88.1 %all-gather.34.cloned.1.call-done = bf16[1408,2048]{1,0:T(8,128)(2,1)} async-done(((bf16[1408,256]{1,0:T(8,128)(2,1)}), bf16[1408,2048]{1,0:T(8,128)(2,1)}) %all-gather.34.cloned.1.call-update) | async-done | bytes 5767184 | tf_op jit(solution)/shard_map/all_gather | solution.py:128
  611.0 115.5 %all-gather.26.cloned.1.call-done = bf16[6,2048,352]{1,2,0:T(8,128)(2,1)} async-done(((bf16[6,256,352]{1,2,0:T(8,128)(2,1)}), bf16[6,2048,352]{1,2,0:T(8,128)(2,1)}) %all-gather.26.cloned.1.call-update) | async-done | bytes 8650768 | tf_op jit(solution)/shard_map/all_gather | solution.py:124
  734.3 121.0 %all-gather.24.cloned.1.call-done = bf16[6,2048,352]{1,2,0:T(8,128)(2,1)} async-done(((bf16[6,256,352]{1,2,0:T(8,128)(2,1)}), bf16[6,2048,352]{1,2,0:T(8,128)(2,1)}) %all-gather.24.cloned.1.call-update) | async-done | bytes 8650768 | tf_op jit(solution)/shard_map/all_gather | solution.py:123
  863.1 120.6 %all-gather.28.cloned.1.call-done = bf16[6,352,2048]{2,1,0:T(8,128)(2,1)} async-done(((bf16[6,352,256]{2,1,0:T(8,128)(2,1)}), bf16[6,352,2048]{2,1,0:T(8,128)(2,1)}) %all-gather.28.cloned.1.call-update) | async-done | bytes 8650768 | tf_op jit(solution)/shard_map/all_gather | solution.py:125
  1127.8 11.3 fusion.7
  1192.2 42.7 %reduce-scatter.39.cloned.1.call-done = f32[16,4]{1,0:T(8,128)} async-done(((f32[128,4]{1,0:T(8,128)}), f32[16,4]{1,0:T(8,128)}) %reduce-scatter.39.cloned.1.call-update) | async-done | bytes 272
  1236.3 64.0 %reduce-scatter.37.cloned.1.call-done = f32[16,4]{1,0:T(8,128)} async-done(((f32[128,4]{1,0:T(8,128)}), f32[16,4]{1,0:T(8,128)}) %reduce-scatter.37.cloned.1.call-update) | async-done | bytes 272
  1301.6 36.8 %all-reduce.9 = (f32[2048]{0:T(1024)S(1)}, f32[2048]{0:T(1024)S(1)}, f32[2048]{0:T(1024)S(1)}) all-reduce(f32[2048]{0:T(1024)S(1)} %get-tuple-element.19, f32[2048]{0:T(1024)S(1)} %get-tuple-element.17, f32[2048]{0:T(1024)S(1)} %bitcast.257), channel_id=2, replica_groups=mesh['dp'=8,'tensor'=4] {'dp'}, use_global_device_ids=true, to_apply=%region_18.19.clone | all-reduce | flops 6144 | bytes 49152
  1347.3 12.3 collective-permute-done.17
  1360.5 38.2 %reduce-scatter.23.cloned.1.call-done = f32[512,256]{1,0:T(8,128)} async-done(((f32[512,2048]{1,0:T(8,128)}), f32[512,256]{1,0:T(8,128)}) %reduce-scatter.23.cloned.1.call-update) | async-done | bytes 524304 | tf_op jit(solution)/shard_map/reduce_scatter | solution.py:348
  1398.7 92.0 %reduce-scatter.17.cloned.1.call-done = f32[256,512]{1,0:T(8,128)} async-done(((f32[2048,512]{1,0:T(8,128)}), f32[256,512]{1,0:T(8,128)}) %reduce-scatter.17.cloned.1.call-update) | async-done | bytes 524304 | tf_op jit(solution)/shard_map/reduce_scatter | solution.py:343
  1490.7 92.2 %reduce-scatter.21.cloned.1.call-done = f32[256,512]{1,0:T(8,128)} async-done(((f32[2048,512]{1,0:T(8,128)}), f32[256,512]{1,0:T(8,128)}) %reduce-scatter.21.cloned.1.call-update) | async-done | bytes 524304 | tf_op jit(solution)/shard_map/reduce_scatter | solution.py:346
  1582.9 92.0 %reduce-scatter.19.cloned.1.call-done = f32[256,512]{1,0:T(8,128)} async-done(((f32[2048,512]{1,0:T(8,128)}), f32[256,512]{1,0:T(8,128)}) %reduce-scatter.19.cloned.1.call-update) | async-done | bytes 524304 | tf_op jit(solution)/shard_map/reduce_scatter | solution.py:345
  1674.9 197.1 %reduce-scatter.35.cloned.1.call-done = f32[1408,256]{1,0:T(8,128)} async-done(((f32[1408,2048]{1,0:T(8,128)}), f32[1408,256]{1,0:T(8,128)}) %reduce-scatter.35.cloned.1.call-update) | async-done | bytes 1441808 | tf_op jit(solution)/shard_map/reduce_scatter | solution.py:338
  1872.0 196.1 %reduce-scatter.33.cloned.1.call-done = f32[256,1408]{1,0:T(8,128)} async-done(((f32[2048,1408]{1,0:T(8,128)}), f32[256,1408]{1,0:T(8,128)}) %reduce-scatter.33.cloned.1.call-update) | async-done | bytes 1441808 | tf_op jit(solution)/shard_map/reduce_scatter | solution.py:337
  2068.1 196.1 %reduce-scatter.31.cloned.1.call-done = f32[256,1408]{1,0:T(8,128)} async-done(((f32[2048,1408]{1,0:T(8,128)}), f32[256,1408]{1,0:T(8,128)}) %reduce-scatter.31.cloned.1.call-update) | async-done | bytes 1441808 | tf_op jit(solution)/shard_map/reduce_scatter | solution.py:336
  2264.3 291.4 %reduce-scatter.29.cloned.1.call-done = f32[6,352,256]{2,1,0:T(8,128)} async-done(((f32[6,352,2048]{2,1,0:T(8,128)}), f32[6,352,256]{2,1,0:T(8,128)}) %reduce-scatter.29.cloned.1.call-update) | async-done | bytes 2162704 | tf_op jit(solution)/shard_map/reduce_scatter | solution.py:335
  2555.7 291.5 %reduce-scatter.27.cloned.1.call-done = f32[6,256,352]{1,2,0:T(8,128)} async-done(((f32[6,2048,352]{1,2,0:T(8,128)}), f32[6,256,352]{1,2,0:T(8,128)}) %reduce-scatter.27.cloned.1.call-update) | async-done | bytes 2162704 | tf_op jit(solution)/shard_map/reduce_scatter | solution.py:334
  2847.2 291.4 %reduce-scatter.25.cloned.1.call-done = f32[6,256,352]{1,2,0:T(8,128)} async-done(((f32[6,2048,352]{1,2,0:T(8,128)}), f32[6,256,352]{1,2,0:T(8,128)}) %reduce-scatter.25.cloned.1.call-update) | async-done | bytes 2162704 | tf_op jit(solution)/shard_map/reduce_scatter | solution.py:333
  (382 shorter events, 338.4 us)
Async XLA Ops:
  7.2 114.9 %all-gather.20.cloned.1.call-start = ((), (), s32[]{:S(2)}) async-start(), calls=%async_computation.14 | async-start | bytes 2359296 | tf_op jit(solution)/shard_map/all_gather | solution.py:107
  9.2 129.0 %all-gather.18.cloned.1.call-start = ((), (), s32[]{:S(2)}) async-start(), calls=%async_computation.13 | async-start | bytes 2359296 | tf_op jit(solution)/shard_map/all_gather | solution.py:105
  11.0 177.5 %all-gather.16.cloned.1.call-start = ((), (), s32[]{:S(2)}) async-start(), calls=%async_computation.12 | async-start | bytes 2359296 | tf_op jit(solution)/shard_map/all_gather | solution.py:108
  11.9 228.1 %all-gather.22.cloned.1.call-start = ((), (), s32[]{:S(2)}) async-start(), calls=%async_computation.15 | async-start | bytes 2359296 | tf_op jit(solution)/shard_map/all_gather | solution.py:110
  15.9 396.8 %all-reduce.15.cloned.1.call-start = ((), (), s32[]{:S(2)}) async-start(), calls=%async_computation.16 | async-start | bytes 3145728 | tf_op jit(solution)/shard_map/psum | solution.py:162
  34.0 63.4 %collective-permute-start.1 = (bf16[128,2048]{1,0:T(8,128)(2,1)S(1)}, bf16[128,2048]{1,0:T(8,128)(2,1)S(1)}, u32[]{:S(2)}, u32[]{:S(2)}) collective-permute-start(bf16[128,2048]{1,0:T(8,128)(2,1)S(1)} %broadcast_select_fusion.1), channel_id=1, source_target_pairs={{0,8},{4,12},{8,16},{12,20},{16,24},{20,28},{24,0},{28,4},{1,9},{5... | collective-permute-start | bytes 1572872 | tf_op jit(solution)/shard_map/ppermute | solution.py:32
  243.3 177.0 %all-gather.30.cloned.1.call-start = ((), (), s32[]{:S(2)}) async-start(), calls=%async_computation.20 | async-start | bytes 6488064 | tf_op jit(solution)/shard_map/all_gather | solution.py:126
  245.6 258.6 %all-gather.32.cloned.1.call-start = ((), (), s32[]{:S(2)}) async-start(), calls=%async_computation.21 | async-start | bytes 6488064 | tf_op jit(solution)/shard_map/all_gather | solution.py:127
  248.1 349.4 %all-gather.34.cloned.1.call-start = ((), (), s32[]{:S(2)}) async-start(), calls=%async_computation.22 | async-start | bytes 6488064 | tf_op jit(solution)/shard_map/all_gather | solution.py:128
  249.1 477.3 %all-gather.26.cloned.1.call-start = ((), (), s32[]{:S(2)}) async-start(), calls=%async_computation.18 | async-start | bytes 9732096 | tf_op jit(solution)/shard_map/all_gather | solution.py:124
  251.9 603.4 %all-gather.24.cloned.1.call-start = ((), (), s32[]{:S(2)}) async-start(), calls=%async_computation.17 | async-start | bytes 9732096 | tf_op jit(solution)/shard_map/all_gather | solution.py:123
  254.8 728.9 %all-gather.28.cloned.1.call-start = ((), (), s32[]{:S(2)}) async-start(), calls=%async_computation.19 | async-start | bytes 9732096 | tf_op jit(solution)/shard_map/all_gather | solution.py:125
  257.7 815.5 %all-reduce.19.cloned.1.call-start = ((), (), s32[]{:S(2)}) async-start(), calls=%async_computation.24 | async-start | bytes 3145728 | tf_op jit(solution)/shard_map/psum | solution.py:262
  259.4 51.2 %collective-permute-start.6 = (s32[128,4]{1,0:T(8,128)S(1)}, s32[128,4]{1,0:T(8,128)S(1)}, u32[]{:S(2)}, u32[]{:S(2)}) collective-permute-start(s32[128,4]{1,0:T(8,128)S(1)} %bitcast.239), channel_id=1, source_target_pairs={{0,4},{4,8},{8,12},{12,16},{16,20},{20,24},{24,28},{28,0},{1,5},{5... | collective-permute-start | bytes 6152 | tf_op jit(solution)/shard_map/ppermute | solution.py:32
  260.3 70.0 %collective-permute-start.12 = (bf16[128,2048]{1,0:T(8,128)(2,1)}, bf16[128,2048]{1,0:T(8,128)(2,1)}, u32[]{:S(2)}, u32[]{:S(2)}) collective-permute-start(bf16[128,2048]{1,0:T(8,128)(2,1)} %get-tuple-element.38), channel_id=1, source_target_pairs={{0,4},{4,8},{8,12},{12,16},{16,20},{20,24},{24,28},{28,0},{1,5},{5... | collective-permute-start | bytes 1572872 | tf_op jit(solution)/shard_map/ppermute | solution.py:32
  355.4 47.2 %collective-permute-start.14 = (bf16[128,2048]{1,0:T(8,128)(2,1)S(1)}, bf16[128,2048]{1,0:T(8,128)(2,1)S(1)}, u32[]{:S(2)}, u32[]{:S(2)}) collective-permute-start(bf16[128,2048]{1,0:T(8,128)(2,1)S(1)} %broadcast_select_fusion.2), channel_id=1, source_target_pairs={{0,16},{4,20},{8,24},{12,28},{16,0},{20,4},{24,8},{28,12},{1,17},{... | collective-permute-start | bytes 1572872 | tf_op jit(solution)/shard_map/ppermute | solution.py:32
  1031.9 131.0 %all-reduce.17.cloned.1.call-start = ((), (), s32[]{:S(2)}) async-start(), calls=%async_computation.23 | async-start | bytes 1572864 | tf_op jit(solution)/shard_map/psum | solution.py:200
  1068.9 95.2 %all-reduce.21.cloned.1.call-start = ((), (), s32[]{:S(2)}) async-start(), calls=%async_computation.25 | async-start | bytes 3145728 | tf_op jit(solution)/shard_map/psum | solution.py:327
  1087.2 147.7 %reduce-scatter.39.cloned.1.call-start = ((), (), s32[]{:S(2)}) async-start(), calls=%async_computation.37 | async-start | bytes 73728
  1088.1 212.2 %reduce-scatter.37.cloned.1.call-start = ((), (), s32[]{:S(2)}) async-start(), calls=%async_computation.36 | async-start | bytes 73728
  1088.9 309.8 %reduce-scatter.23.cloned.1.call-start = ((), (), s32[]{:S(2)}) async-start(), calls=%async_computation.29 | async-start | bytes 4718592 | tf_op jit(solution)/shard_map/reduce_scatter | solution.py:348
  1093.0 397.7 %reduce-scatter.17.cloned.1.call-start = ((), (), s32[]{:S(2)}) async-start(), calls=%async_computation.26 | async-start | bytes 4718592 | tf_op jit(solution)/shard_map/reduce_scatter | solution.py:343
  1096.8 486.1 %reduce-scatter.21.cloned.1.call-start = ((), (), s32[]{:S(2)}) async-start(), calls=%async_computation.28 | async-start | bytes 4718592 | tf_op jit(solution)/shard_map/reduce_scatter | solution.py:346
  1100.6 574.3 %reduce-scatter.19.cloned.1.call-start = ((), (), s32[]{:S(2)}) async-start(), calls=%async_computation.27 | async-start | bytes 4718592 | tf_op jit(solution)/shard_map/reduce_scatter | solution.py:345
  1104.3 767.7 %reduce-scatter.35.cloned.1.call-start = ((), (), s32[]{:S(2)}) async-start(), calls=%async_computation.35 | async-start | bytes 12976128 | tf_op jit(solution)/shard_map/reduce_scatter | solution.py:338
  1112.5 955.6 %reduce-scatter.33.cloned.1.call-start = ((), (), s32[]{:S(2)}) async-start(), calls=%async_computation.34 | async-start | bytes 12976128 | tf_op jit(solution)/shard_map/reduce_scatter | solution.py:337
  1119.6 1144.7 %reduce-scatter.31.cloned.1.call-start = ((), (), s32[]{:S(2)}) async-start(), calls=%async_computation.33 | async-start | bytes 12976128 | tf_op jit(solution)/shard_map/reduce_scatter | solution.py:336
  1126.8 1428.9 %reduce-scatter.29.cloned.1.call-start = ((), (), s32[]{:S(2)}) async-start(), calls=%async_computation.32 | async-start | bytes 19464192 | tf_op jit(solution)/shard_map/reduce_scatter | solution.py:335
  1139.1 1708.1 %reduce-scatter.27.cloned.1.call-start = ((), (), s32[]{:S(2)}) async-start(), calls=%async_computation.31 | async-start | bytes 19464192 | tf_op jit(solution)/shard_map/reduce_scatter | solution.py:334
  1149.5 1989.0 %reduce-scatter.25.cloned.1.call-start = ((), (), s32[]{:S(2)}) async-start(), calls=%async_computation.30 | async-start | bytes 19464192 | tf_op jit(solution)/shard_map/reduce_scatter | solution.py:333
  1184.6 161.7 %collective-permute-start.16 = (f32[128,512]{1,0:T(8,128)S(1)}, f32[128,512]{1,0:T(8,128)S(1)}, u32[]{:S(2)}, u32[]{:S(2)}) collective-permute-start(f32[128,512]{1,0:T(8,128)S(1)} %broadcast_select_fusion.6), channel_id=1, source_target_pairs={{0,24},{4,28},{8,0},{12,4},{16,8},{20,12},{24,16},{28,20},{1,25},{... | collective-permute-start | bytes 786440 | tf_op jit(solution)/shard_map/ppermute | solution.py:32
  1190.3 156.1 %collective-permute-start.11 = (f32[128,512]{1,0:T(8,128)S(1)}, f32[128,512]{1,0:T(8,128)S(1)}, u32[]{:S(2)}, u32[]{:S(2)}) collective-permute-start(f32[128,512]{1,0:T(8,128)S(1)} %broadcast_select_fusion.9), channel_id=1, source_target_pairs={{0,16},{4,20},{8,24},{12,28},{16,0},{20,4},{24,8},{28,12},{1,17},{... | collective-permute-start | bytes 786440 | tf_op jit(solution)/shard_map/ppermute | solution.py:32
  (73 other events, 880.2 us)
Sparse Core Ops, SparseCore 0:
  10.7 64.4 all-gather.19
  77.9 60.1 all-gather.17
  140.9 47.6 all-gather.15
  191.0 48.8 all-gather.21
  243.4 41.0 all-reduce.14
  287.1 124.6 all-gather.29
  414.5 89.5 all-gather.31
  506.2 91.2 all-gather.33
  600.1 126.2 all-gather.25
  728.9 126.3 all-gather.23
  857.4 126.3 all-gather.27
  1032.0 41.0 all-reduce.18
  1075.5 34.8 all-reduce.16
  1112.6 43.0 all-reduce.20
  1158.9 75.9 reduce-scatter.38
  1238.7 61.4 reduce-scatter.36
  1304.3 94.3 reduce-scatter.22
  1402.7 87.9 reduce-scatter.16
  1494.9 87.9 reduce-scatter.20
  1586.9 87.9 reduce-scatter.18
  1679.1 192.8 reduce-scatter.34
  1876.2 191.9 reduce-scatter.32
  2072.3 191.9 reduce-scatter.30
  2268.6 287.0 reduce-scatter.28
  2560.2 286.9 reduce-scatter.26
  2851.5 286.9 reduce-scatter.24
where the time goes:
time: 3150 us
  waiting for transfers between devices  2660 us (84%)
  blocking collectives  154 us (5%)
  matrix products  153 us (5%)
  local copies, waits for them, and re-layouts  95.9 us (3%)
  other arithmetic  43.3 us (1%)
    reduce_scatter x1, waiting for transfers between devices, per_device(): lax.psum_scatter(grad_up_experts, 'dp', scatter_dimension=1, tiled=True)  291 us
    reduce_scatter x1, waiting for transfers between devices, per_device(): lax.psum_scatter(grad_down_experts, 'dp', scatter_dimension=2, tiled=True)  291 us
    reduce_scatter x1, waiting for transfers between devices, per_device(): lax.psum_scatter(grad_gate_experts, 'dp', scatter_dimension=1, tiled=True)  291 us
    reduce_scatter x1, waiting for transfers between devices, per_device(): lax.psum_scatter(grad_down_shared, 'dp', scatter_dimension=1, tiled=True)  197 us
    reduce_scatter x1, waiting for transfers between devices, per_device(): lax.psum_scatter(grad_gate_shared, 'dp', scatter_dimension=0, tiled=True)  196 us
    reduce_scatter x1, waiting for transfers between devices, per_device(): lax.psum_scatter(grad_up_shared, 'dp', scatter_dimension=0, tiled=True)  196 us
    ppermute x18, waiting for transfers between devices, shifted(): return lax.ppermute(value, axis, pairs)  140 us
    all_gather x1, waiting for transfers between devices, per_device(): lax.all_gather(expert_gate.astype(jnp.bfloat16), 'dp', axis=1, tiled=True)  121 us
  transfers between devices with their start and end apart: 44, of which 31 were waited for; matrix products, arithmetic and copies ran while one was open for 7% of the time, Pallas kernels for 0%

commit v1 on v0

v1 whole, which is shorter than its diff:
```python
from functools import partial

import jax
import jax.numpy as jnp
from jax import lax
from jax.sharding import PartitionSpec as P

HEAD_DIM = 128
EPSILON = 1e-06
NEGATIVE = -1e30
LANES = 128
BF16 = jnp.bfloat16
F32 = jnp.float32
ALL = ("dp", "tensor")


def normalize(values, gain):
    return values * lax.rsqrt(jnp.mean(values * values, axis=-1, keepdims=True) + EPSILON) * gain


def nt(left, right):
    return lax.dot_general(left, right, (((1,), (1,)), ((), ())), preferred_element_type=F32)


def tn(left, right):
    return lax.dot_general(left, right, (((0,), (0,)), ((), ())), preferred_element_type=F32)


def nn(left, right):
    return lax.dot_general(left, right, (((1,), (0,)), ((), ())), preferred_element_type=F32)


def gather_all(value):
    return lax.all_gather(value, ALL, axis=0, tiled=True)


def scatter_all(value):
    return lax.psum_scatter(value, ALL, scatter_dimension=0, tiled=True)


def exchange_dp(value):
    return lax.all_to_all(value, "dp", 0, 0, tiled=False)


def per_device(
    tokens,
    cotangent,
    routes,
    gates,
    lengths,
    deal,
    norm1_gain,
    q_weight,
    q_bias,
    k_weight,
    v_weight,
    v_bias,
    o_weight,
    norm2_gain,
    expert_gate,
    expert_up,
    expert_down,
    shared_gate,
    shared_up,
    shared_down,
    shared_switch,
):
    n_dp = lax.axis_size("dp")
    n_tensor = lax.axis_size("tensor")
    place = lax.axis_index("dp")
    member = lax.axis_index("tensor")
    seqs, span, width = tokens.shape
    rows = seqs * span
    shard = rows // n_tensor
    experts, slice_d, expert_cols = expert_gate.shape
    shared_cols = shared_gate.shape[1]
    head_cols = q_weight.shape[1]
    heads = head_cols // HEAD_DIM

    def own_rows(value):
        return lax.dynamic_slice_in_dim(value, member * shard, shard, 0)

    valid = (jnp.arange(span)[None, :] < lengths[:, None]).reshape(rows, 1)
    dense = jnp.zeros((seqs, span, LANES), F32)
    for rank in range(routes.shape[-1]):
        hit = routes[..., rank, None] == jnp.arange(LANES)
        dense = dense + jnp.where(hit, gates[..., rank, None].astype(F32), 0.0)
    dense = dense.reshape(rows, LANES).astype(BF16)
    cot = jnp.where(valid, cotangent.reshape(rows, width), 0).astype(BF16)
    cot_packed = gather_all(own_rows(jnp.concatenate([cot, dense], axis=1)))

    small = jnp.concatenate(
        [norm1_gain, norm2_gain, shared_switch, q_bias.reshape(-1), v_bias.reshape(-1)]
    ).astype(BF16)
    small = lax.all_gather(small[None, :], "dp", axis=0, tiled=True)
    gain_one = small[:, :slice_d].reshape(-1).astype(F32)
    gain_two = small[:, slice_d : 2 * slice_d].reshape(-1).astype(F32)
    switch = small[:, 2 * slice_d : 3 * slice_d].reshape(1, -1)
    piece = q_bias.shape[1]

    def whole_bias(start):
        part = small[:, start : start + heads * piece].reshape(n_dp, heads, piece)
        return part.transpose(1, 0, 2).reshape(-1).astype(F32)

    bias_q = whole_bias(3 * slice_d)
    bias_v = whole_bias(3 * slice_d + heads * piece)
    attn_weights = jnp.concatenate(
        [q_weight.astype(BF16), k_weight.astype(BF16), v_weight.astype(BF16), o_weight.T.astype(BF16)],
        axis=1,
    )
    attn_weights = lax.all_gather(attn_weights, "dp", axis=0, tiled=True)
    weight_qkv = attn_weights[:, : 3 * head_cols]
    weight_o = attn_weights[:, 3 * head_cols :]

    def by_unit(expert_part, shared_part):
        return jnp.concatenate(
            [
                expert_part.astype(BF16).reshape(n_dp, -1, slice_d),
                shared_part.astype(BF16).reshape(n_dp, -1, slice_d),
            ],
            axis=1,
        )

    gate_sent = by_unit(
        expert_gate.astype(BF16).transpose(0, 2, 1).reshape(-1, slice_d), shared_gate.astype(BF16).T
    )
    up_sent = by_unit(
        expert_up.astype(BF16).transpose(0, 2, 1).reshape(-1, slice_d), shared_up.astype(BF16).T
    )
    down_sent = by_unit(expert_down.reshape(-1, slice_d), shared_down)
    arrived = exchange_dp(jnp.stack([gate_sent, up_sent, down_sent], axis=1))
    units = arrived.shape[2]
    routed = experts * expert_cols // n_dp
    arrived = arrived.transpose(1, 2, 0, 3).reshape(3, units, width)
    gate_units, up_units, down_units = arrived[0], arrived[1], arrived[2]

    inputs = tokens.reshape(rows, width).astype(F32)
    inputs_own = own_rows(inputs)
    normed_one = normalize(inputs, gain_one).astype(BF16)
    projected = nn(normed_one, weight_qkv)
    head_shape = (seqs, span, heads, HEAD_DIM)
    queries = (projected[:, :head_cols] + bias_q).astype(BF16).reshape(head_shape)
    keys = projected[:, head_cols : 2 * head_cols].astype(BF16).reshape(head_shape)
    values = (projected[:, 2 * head_cols :] + bias_v).astype(BF16).reshape(head_shape)
    order = jnp.arange(span)
    causal = order[None, :] <= order[:, None]
    scale = HEAD_DIM ** (-0.5)
    scores = jnp.einsum("bqhd,bkhd->bhqk", queries, keys, preferred_element_type=F32) * scale
    scores = jnp.where(causal, scores, NEGATIVE)
    top = jnp.max(scores, axis=-1, keepdims=True)
    powers = jnp.exp(scores - top)
    probs = powers / jnp.sum(powers, axis=-1, keepdims=True)
    probs_low = probs.astype(BF16)
    attended = (
        jnp.einsum("bhqk,bkhd->bqhd", probs_low, values, preferred_element_type=F32)
        .reshape(rows, -1)
        .astype(BF16)
    )
    attn_part = nt(attended, weight_o)
    middle = inputs_own + lax.psum_scatter(attn_part, "tensor", scatter_dimension=0, tiled=True)

    normed_two = gather_all(normalize(middle, gain_two).astype(BF16))
    cot_all = cot_packed[:, :width]
    route_share = cot_packed[:, width : width + LANES]
    unit_expert = (place * routed + jnp.arange(routed)) // expert_cols
    picks = (jnp.arange(LANES)[:, None] == unit_expert[None, :]).astype(BF16)
    gate_logit = nt(normed_two, switch)
    switch_gate = jax.nn.sigmoid(gate_logit)
    share = jnp.concatenate(
        [nn(route_share, picks), jnp.broadcast_to(switch_gate, (switch_gate.shape[0], units - routed))],
        axis=1,
    )
    gate_act = nt(normed_two, gate_units)
    up_act = nt(normed_two, up_units)
    logistic = jax.nn.sigmoid(gate_act)
    silu = gate_act * logistic
    inner = (silu * up_act).astype(BF16).astype(F32)
    inner_share = (inner * share).astype(BF16)
    mixed = nn(inner_share, down_units).astype(BF16)
    mixed = lax.psum_scatter(mixed, "dp", scatter_dimension=0, tiled=True)
    mixed = lax.psum_scatter(mixed, "tensor", scatter_dimension=1, tiled=True)

    grad_inner_raw = nt(cot_all, down_units)
    grad_logit = (
        jnp.sum(inner[:, routed:] * grad_inner_raw[:, routed:], axis=1, keepdims=True)
        * switch_gate
        * (1.0 - switch_gate)
    )
    grad_inner = grad_inner_raw * share
    slope = logistic * (1.0 + gate_act * (1.0 - logistic))
    grad_gate_act = (grad_inner * up_act * slope).astype(BF16)
    grad_up_act = (grad_inner * silu).astype(BF16)
    back_two = nn(grad_gate_act, gate_units) + nn(grad_up_act, up_units)
    back_two = (back_two + grad_logit * switch.astype(F32)).astype(BF16)
    back_two = scatter_all(back_two).astype(F32)
    grad_down = tn(inner_share, cot_all)
    grad_gate = tn(grad_gate_act, normed_two)
    grad_up = tn(grad_up_act, normed_two)
    grad_switch = jnp.sum(grad_logit * normed_two.astype(F32), axis=0)
    sent_back = jnp.stack([grad_gate, grad_up, grad_down]).astype(BF16)
    sent_back = sent_back.reshape(3, units, n_dp, slice_d).transpose(2, 0, 1, 3)
    returned = exchange_dp(sent_back).astype(F32)

    def split_units(value):
        routed_part = value[:, :routed].reshape(experts, expert_cols, slice_d)
        return routed_part, value[:, routed:].reshape(shared_cols, slice_d)

    grad_gate_experts, grad_gate_shared = split_units(returned[:, 0])
    grad_up_experts, grad_up_shared = split_units(returned[:, 1])
    grad_down_experts, grad_down_shared = split_units(returned[:, 2])

    unused_two, norm_two_back = jax.vjp(normalize, middle, gain_two)
    grad_middle_norm, grad_gain_two = norm_two_back(back_two)
    grad_middle = own_rows(cot).astype(F32) + grad_middle_norm
    grad_attn = lax.all_gather(grad_middle.astype(BF16), "tensor", axis=0, tiled=True)
    grad_weight_o = tn(grad_attn, attended)
    grad_attended = nn(grad_attn, weight_o).astype(BF16).reshape(head_shape)
    grad_values = (
        jnp.einsum("bhqk,bqhd->bkhd", probs_low, grad_attended, preferred_element_type=F32)
        .astype(BF16)
        .reshape(rows, -1)
    )
    grad_probs = jnp.einsum("bqhd,bkhd->bhqk", grad_attended, values, preferred_element_type=F32)
    grad_scores = (
        probs * (grad_probs - jnp.sum(grad_probs * probs, axis=-1, keepdims=True))
    ).astype(BF16)
    grad_queries = (
        (jnp.einsum("bhqk,bkhd->bqhd", grad_scores, keys, preferred_element_type=F32) * scale)
        .astype(BF16)
        .reshape(rows, -1)
    )
    grad_keys = (
        (jnp.einsum("bhqk,bqhd->bkhd", grad_scores, queries, preferred_element_type=F32) * scale)
        .astype(BF16)
        .reshape(rows, -1)
    )
    grad_qkv = jnp.concatenate([grad_queries, grad_keys, grad_values], axis=1)
    grad_attn_weights = jnp.concatenate([tn(normed_one, grad_qkv), grad_weight_o], axis=1).astype(BF16)
    grad_attn_weights = lax.psum_scatter(
        grad_attn_weights, "dp", scatter_dimension=0, tiled=True
    ).astype(F32)
    back_one = nt(grad_qkv, weight_qkv)
    back_one = lax.psum_scatter(back_one, "tensor", scatter_dimension=0, tiled=True)
    unused_one, norm_one_back = jax.vjp(normalize, inputs_own, gain_one)
    grad_input_norm, grad_gain_one = norm_one_back(back_one)
    grad_input = grad_middle + grad_input_norm

    bias_part = jnp.concatenate(
        [
            jnp.sum(grad_queries.astype(F32), axis=0).reshape(heads, n_dp, piece),
            jnp.sum(grad_values.astype(F32), axis=0).reshape(heads, n_dp, piece),
        ],
        axis=0,
    )
    bias_part = bias_part.transpose(1, 0, 2).reshape(1, n_dp, -1)
    mine = (jnp.arange(n_tensor) == member)[:, None, None]
    bias_part = jnp.where(mine, bias_part, 0.0)
    gains = jnp.concatenate([grad_gain_one, grad_gain_two, grad_switch])
    gains = gains.reshape(1, 3, n_dp, slice_d).transpose(0, 2, 1, 3).reshape(n_dp, 3 * slice_d)
    pack = jnp.concatenate([gains, bias_part.transpose(1, 0, 2).reshape(n_dp, -1)], axis=1)
    pack = lax.psum(pack, ALL)
    pack = lax.dynamic_slice_in_dim(pack, place, 1, 0)[0]
    bias_own = lax.dynamic_slice_in_dim(
        pack[3 * slice_d :].reshape(n_tensor, 2, heads, piece), member, 1, 0
    )[0]

    def to_columns(value):
        return lax.all_to_all(value, "tensor", 1, 0, tiled=True)

    out_shape = (seqs, span, width // n_tensor)
    output = jnp.where(valid, to_columns(middle) + mixed.astype(F32), 0.0).reshape(out_shape)
    tokens_grad = jnp.where(valid, to_columns(grad_input), 0.0).reshape(out_shape)
    return (
        output,
        tokens_grad,
        pack[:slice_d],
        grad_attn_weights[:, :head_cols],
        bias_own[0],
        grad_attn_weights[:, head_cols : 2 * head_cols],
        grad_attn_weights[:, 2 * head_cols : 3 * head_cols],
        bias_own[1],
        grad_attn_weights[:, 3 * head_cols :].T,
        pack[slice_d : 2 * slice_d],
        grad_gate_experts.transpose(0, 2, 1),
        grad_up_experts.transpose(0, 2, 1),
        grad_down_experts,
        grad_gate_shared.T,
        grad_up_shared.T,
        grad_down_shared,
        pack[2 * slice_d : 3 * slice_d],
    )


IN_SPECS = (
    P("dp", None, None),
    P("dp", None, None),
    P("dp", None, None),
    P("dp", None, None),
    P("dp"),
    P(),
    P("dp"),
    P("dp", "tensor"),
    P("tensor", "dp"),
    P("dp", "tensor"),
    P("dp", "tensor"),
    P("tensor", "dp"),
    P("tensor", "dp"),
    P("dp"),
    P(None, "dp", "tensor"),
    P(None, "dp", "tensor"),
    P(None, "tensor", "dp"),
    P("dp", "tensor"),
    P("dp", "tensor"),
    P("tensor", "dp"),
    P("dp"),
)
OUT_SPECS = (P("dp", None, "tensor"), P("dp", None, "tensor")) + IN_SPECS[6:]


def solution(mesh):
    return jax.shard_map(
        per_device, mesh=mesh, in_specs=IN_SPECS, out_specs=OUT_SPECS, check_vma=False
    )
```

time: 3150 us -> 1110 us (0.35)
  waiting for transfers between devices: 2660 us -> 770 us
  blocking collectives: 154 us -> 74.8 us
  matrix products: 153 us -> 111 us
    reduce_scatter x10 -> x6, waiting for transfers between devices: 1780 us -> 309 us  [the longest x1 144 us: per_device(): mixed = lax.psum_scatter(mixed, 'dp', scatter_dimension=0, tiled=True)]
    all_gather x10 -> x4, waiting for transfers between devices: 634 us -> 136 us  [the longest x1 91.7 us: per_device(): attn_weights = lax.all_gather(attn_weights, 'dp', axis=0, tiled=True)]
    all_to_all x0 -> x4, waiting for transfers between devices: none -> 325 us  [the longest x2 325 us: exchange_dp(): return lax.all_to_all(value, 'dp', 0, 0, tiled=False)]
    ppermute x18 -> x0, waiting for transfers between devices: 140 us -> none  [shifted(): return lax.ppermute(value, axis, pairs)]
    unnamed x28 -> x10, waiting for transfers between devices: 107 us -> 0.17 us
    all_gather x5 -> x1, blocking collectives: 111 us -> 33.5 us  [per_device(): small = lax.all_gather(small[None, :], 'dp', axis=0, tiled=True)]
    gather x10 -> x0, local copies, waits for them, and re-layouts: 55.7 us -> none  [the longest x4 23.4 us: per_device(): expert_out[slot_grid[:, rank_slot]]]
    dot_general x38 -> x23, matrix products: 153 us -> 111 us  [the longest x6 40.1 us: nn(): lax.dot_general(left, right, (((1,), (0,)), ((), ())), preferred_element_...]
  transfers between devices with their start and end apart: 44 -> 14, of which waited for: 31 -> 7; matrix products, arithmetic and copies ran while one was open for 7% -> 13% of each run, Pallas kernels for 0% -> 0%
where the time goes in v1:
time: 1110 us; the launch traced here: 1100 us
  waiting for transfers between devices  770 us (69%)
  matrix products  111 us (10%)
  blocking collectives  74.8 us (7%)
  local copies, waits for them, and re-layouts  66.3 us (6%)
  other arithmetic  47.6 us (4%)
  starting transfers between devices  18.5 us (2%)
  between operations  16.9 us (2%)
    all_to_all x2, waiting for transfers between devices, exchange_dp(): return lax.all_to_all(value, 'dp', 0, 0, tiled=False)  325 us
    reduce_scatter x1, waiting for transfers between devices, per_device(): mixed = lax.psum_scatter(mixed, 'dp', scatter_dimension=0, tiled=True)  144 us
    reduce_scatter x1, waiting for transfers between devices, scatter_all(): return lax.psum_scatter(value, ALL, scatter_dimension=0, tiled=True)  139 us
    all_gather x1, waiting for transfers between devices, per_device(): attn_weights = lax.all_gather(attn_weights, 'dp', axis=0, tiled=True)  91.7 us
    all_gather x2, waiting for transfers between devices, gather_all(): return lax.all_gather(value, ALL, axis=0, tiled=True)  44.5 us
    psum x1, blocking collectives, per_device(): pack = lax.psum(pack, ALL)  41.3 us
    dot_general x6, matrix products, nn(): lax.dot_general(left, right, (((1,), (0,)), ((), ())), preferred_element_...  40.1 us
    dot_general x6, matrix products, nt(): lax.dot_general(left, right, (((1,), (1,)), ((), ())), preferred_element_...  38.7 us
  transfers between devices with their start and end apart: 14, of which 7 were waited for; matrix products, arithmetic and copies ran while one was open for 13% of the time, Pallas kernels for 0%

profile of v1, /device:TPU:0, one launch (start us, length us, event | category | flops | bytes accessed | tf_op | source)
XLA Modules:
  0.0 1104.9 jit_solution(10503144483082694511)
XLA Ops:
  13.3 33.5 %all-gather = bf16[8,1,896]{2,1,0:T(2,128)(2,1)S(1)} all-gather(bf16[1,1,896]{2,1,0:T(2,128)(2,1)S(1)} %bitcast.258), channel_id=1, replica_groups=mesh['dp'=8,'tensor'=4] {'dp'}, dimensions={0}, use_global_device_ids=true | all-gather | bytes 16128 | tf_op jit(solution)/shard_map/all_gather | solution.py:95
  49.2 91.7 %all-gather.6.cloned.1.call-done = bf16[2048,2048]{0,1:T(8,128)(2,1)} async-done(((bf16[256,2048]{0,1:T(8,128)(2,1)}), bf16[2048,2048]{0,1:T(8,128)(2,1)}) %all-gather.6.cloned.1.call-update) | async-done | bytes 8388624 | tf_op jit(solution)/shard_map/all_gather | solution.py:111
  140.9 4.6 fusion.7
  149.5 3.6 fusion.18
  156.4 26.3 %reduce-scatter.7.cloned.1.call-done = f32[64,2048]{1,0:T(8,128)} async-done(((f32[256,2048]{1,0:T(8,128)}), f32[64,2048]{1,0:T(8,128)}) %reduce-scatter.7.cloned.1.call-update) | async-done | bytes 524304 | tf_op jit(solution)/shard_map/reduce_scatter | solution.py:160
  200.5 5.5 all-to-all-start.1
  206.3 145.4 %all-to-all-done.1 = bf16[8,3,440,256]{3,2,1,0:T(8,128)(2,1)} async-done(((bf16[8,3,440,256]{3,2,1,0:T(8,128)(2,1)}), bf16[8,3,440,256]{3,2,1,0:T(8,128)(2,1)}, u32[]{:S(2)}, u32[]{:S(2)}) %all-to-all-start.1) | async-done | bytes 5406752 | tf_op jit(solution)/shard_map/all_to_all | solution.py:42
  361.9 44.5 %all-gather.8.cloned.1.call-done = bf16[2048,2048]{1,0:T(8,128)(2,1)} async-done(((bf16[64,2048]{1,0:T(8,128)(2,1)}), bf16[2048,2048]{1,0:T(8,128)(2,1)}) %all-gather.8.cloned.1.call-update) | async-done | bytes 8388624 | tf_op jit(solution)/shard_map/all_gather | solution.py:34
  406.4 5.8 fusion.73
  412.6 5.7 fusion.72
  418.3 5.8 fusion.71
  424.3 11.5 %multiply_convert_fusion = (bf16[2048,440]{0,1:T(8,128)(2,1)}, bf16[2048,440]{0,1:T(8,128)(2,1)S(1)}, bf16[2048,440]{0,1:T(8,128)(2,1)}, f32[2048,440]{0,1:T(8,128)}, f32[2048,440]{0,1:T(8,128)}) fusion(f32[2048,176]{0,1:T(8,128)S(1)} %broadcast_in_dim.169, f32[2048,264]{0,1:T(8,128)S(1)} %copy-done.11, f32[2048,440]{0,1:T(8,128)} %fusion.71, ...), kind=kOutput, calls=%fused_computation.24 | convolution fusion | flops 3709009920 | bytes 33619968 | tf_op jit(solution)/shard_map/dot_general | solution.py:22
  438.5 8.2 fusion.74
  446.6 11.2 %add_convert_fusion = bf16[2048,2048]{1,0:T(8,128)(2,1)} fusion(f32[2048,2048]{1,0:T(8,128)} %fusion.74, f32[2048]{0:T(1024)S(1)} %convert_element_type.270, f32[2048]{0:T(1024)S(1)} %subtract_multiply_fusion, bf16[2048,440]{0,1:T(8,128)(2,1)} %get-tuple-element.98, bf16[440,2048]{1,0:T(8,128)(2,1)S(1)} %bitcast.231), kind=kOutput, calls=%fused_computation.2 | convolution fusion | flops 3707764736 | bytes 28786688 | tf_op jit(solution)/shard_map/dot_general | solution.py:30
  458.4 9.9 convolution_convert_fusion.1
  468.3 138.6 %reduce-scatter.13.cloned.1.call-done = bf16[64,2048]{1,0:T(8,128)(2,1)} async-done(((bf16[2048,2048]{1,0:T(8,128)(2,1)}), bf16[64,2048]{1,0:T(8,128)(2,1)}) %reduce-scatter.13.cloned.1.call-update) | async-done | bytes 262160 | tf_op jit(solution)/shard_map/reduce_scatter | solution.py:38
  610.1 143.7 %reduce-scatter.9.cloned.1.call-done = bf16[256,2048]{1,0:T(8,128)(2,1)} async-done(((bf16[2048,2048]{1,0:T(8,128)(2,1)}), bf16[256,2048]{1,0:T(8,128)(2,1)}) %reduce-scatter.9.cloned.1.call-update) | async-done | bytes 1048592 | tf_op jit(solution)/shard_map/reduce_scatter | solution.py:180
  753.8 3.4 fusion.25
  767.8 6.2 fusion.5
  777.6 4.5 convolution_convert_fusion
  782.2 8.4 pad_maximum_fusion
  790.6 7.8 fusion.13
  800.8 7.5 convolution_convert_fusion.4
  810.3 4.1 convolution_convert_fusion.3
  818.3 4.9 all-to-all-start.3
  824.1 5.1 multiply_reduce_fusion
  829.2 179.2 %all-to-all-done.3 = bf16[8,3,440,256]{3,2,1,0:T(8,128)(2,1)} async-done(((bf16[8,3,440,256]{3,2,1,0:T(8,128)(2,1)}), bf16[8,3,440,256]{3,2,1,0:T(8,128)(2,1)}, u32[]{:S(2)}, u32[]{:S(2)}) %all-to-all-start.3) | async-done | bytes 5406752 | tf_op jit(solution)/shard_map/all_to_all | solution.py:42
  1008.4 3.5 all-to-all-start
  1011.9 3.5 copy_convert_fusion
  1015.4 4.2 slice_bitcast_fusion
  1044.7 3.5 all-to-all-start.2
  1048.2 41.3 %psum.7 = f32[8,1280]{1,0:T(8,128)S(1)} all-reduce(f32[8,1280]{1,0:T(8,128)S(1)} %pad_maximum_fusion.4), channel_id=1, replica_groups=mesh['dp'=8,'tensor'=4] {'dp','tensor'}, use_global_device_ids=true, to_apply=%region_19.20 | all-reduce | flops 10240 | bytes 81920 | tf_op jit(solution)/shard_map/psum | solution.py:261
  (244 shorter events, 105.4 us)
Async XLA Ops:
  8.0 132.9 %all-gather.6.cloned.1.call-start = ((), (), s32[]{:S(2)}) async-start(), calls=%async_computation.10 | async-start | bytes 9437184 | tf_op jit(solution)/shard_map/all_gather | solution.py:111
  11.7 35.6 %copy-start.4 = (bf16[2,128,2048]{2,1,0:T(8,128)(2,1)S(1)}, bf16[2,128,2048]{2,1,0:T(8,128)(2,1)}, u32[]{:S(2)}) copy-start(bf16[2,128,2048]{2,1,0:T(8,128)(2,1)} %param.21) | copy-start | bytes 3145732
  12.8 169.9 %reduce-scatter.7.cloned.1.call-start = ((), (), s32[]{:S(2)}) async-start(), calls=%async_computation.11 | async-start | bytes 2621440 | tf_op jit(solution)/shard_map/reduce_scatter | solution.py:160
  148.0 5.2 copy-start.12
  149.5 3.8 copy-start.36
  149.5 4.3 copy-start.25
  149.5 4.3 copy-start.26
  153.2 205.8 %all-gather.10.cloned.1.call-start = ((), (), s32[]{:S(2)}) async-start(), calls=%async_computation.13 | async-start | bytes 9191424 | tf_op jit(solution)/shard_map/all_gather | solution.py:34
  153.8 28.9 %copy-start.27 = (pred[256]{0:T(512)(128)(4,1)}, pred[256]{0:T(512)(128)(4,1)S(1)}, u32[]{:S(2)}) copy-start(pred[256]{0:T(512)(128)(4,1)S(1)} %get-tuple-element.131) | copy-start | bytes 772
  156.4 250.0 %all-gather.8.cloned.1.call-start = ((), (), s32[]{:S(2)}) async-start(), calls=%async_computation.12 | async-start | bytes 8650752 | tf_op jit(solution)/shard_map/all_gather | solution.py:34
  200.5 151.3 %all-to-all-start.1 = ((bf16[8,3,440,256]{3,2,1,0:T(8,128)(2,1)}), bf16[8,3,440,256]{3,2,1,0:T(8,128)(2,1)}, u32[]{:S(2)}, u32[]{:S(2)}) async-start(bf16[8,3,440,256]{3,2,1,0:T(8,128)(2,1)} %pad_maximum_fusion.1), calls=%async_computation.2 | async-start | bytes 10813440 | tf_op jit(solution)/shard_map/all_to_all | solution.py:42
  206.0 400.9 %reduce-scatter.13.cloned.1.call-start = ((), (), s32[]{:S(2)}) async-start(), calls=%async_computation.16 | async-start | bytes 8650752 | tf_op jit(solution)/shard_map/reduce_scatter | solution.py:38
  406.4 5.8 copy-start
  406.4 6.3 copy-start.15
  412.6 5.7 copy-start.16
  418.3 6.0 copy-start.11
  418.3 6.0 copy-start.14
  435.8 10.8 copy-start.37
  457.9 295.8 %reduce-scatter.9.cloned.1.call-start = ((), (), s32[]{:S(2)}) async-start(), calls=%async_computation.14 | async-start | bytes 9437184 | tf_op jit(solution)/shard_map/reduce_scatter | solution.py:180
  468.3 285.6 %all-gather.12.cloned.1.call-start = ((), (), s32[]{:S(2)}) async-start(), calls=%async_computation.17 | async-start | bytes 1310720 | tf_op jit(solution)/shard_map/all_gather | solution.py:215
  610.0 428.9 %reduce-scatter.11.cloned.1.call-start = ((), (), s32[]{:S(2)}) async-start(), calls=%async_computation.15 | async-start | bytes 1310720 | tf_op jit(solution)/shard_map/reduce_scatter | solution.py:181
  753.8 287.0 %reduce-scatter.15.cloned.1.call-start = ((), (), s32[]{:S(2)}) async-start(), calls=%async_computation.18 | async-start | bytes 2621440 | tf_op jit(solution)/shard_map/reduce_scatter | solution.py:243
  774.0 317.8 %reduce-scatter.17.cloned.1.call-start = ((), (), s32[]{:S(2)}) async-start(), calls=%async_computation.19 | async-start | bytes 9437184 | tf_op jit(solution)/shard_map/reduce_scatter | solution.py:239
  798.4 10.8 slice-start
  800.8 8.4 slice-start.1
  818.3 5.8 copy-start.31
  818.3 190.1 %all-to-all-start.3 = ((bf16[8,3,440,256]{3,2,1,0:T(8,128)(2,1)}), bf16[8,3,440,256]{3,2,1,0:T(8,128)(2,1)}, u32[]{:S(2)}, u32[]{:S(2)}) async-start(bf16[8,3,440,256]{3,2,1,0:T(8,128)(2,1)} %maximum_bitcast_fusion), calls=%async_computation.9 | async-start | bytes 10813440 | tf_op jit(solution)/shard_map/all_to_all | solution.py:42
  1008.4 30.5 %all-to-all-start = ((f32[64,4,512]{2,0,1:T(8,128)}), f32[64,4,512]{2,0,1:T(8,128)S(1)}, u32[]{:S(2)}, u32[]{:S(2)}) async-start(f32[64,4,512]{2,0,1:T(8,128)} %bitcast.197), calls=%async_computation.1 | async-start | bytes 1048576 | tf_op jit(solution)/shard_map/all_to_all | solution.py:268
  1035.6 5.2 copy-start.24
  1035.6 6.7 copy-start.7
  1042.3 48.6 %copy-start.32 = (pred[2,128]{1,0:T(4,128)(4,1)S(1)}, pred[2,128]{1,0:T(4,128)(4,1)}, u32[]{:S(2)}) copy-start(pred[2,128]{1,0:T(4,128)(4,1)} %get-tuple-element.130) | copy-start | bytes 772
  1044.7 46.2 %all-to-all-start.2 = ((f32[64,4,512]{2,0,1:T(8,128)}), f32[64,4,512]{2,0,1:T(8,128)S(1)}, u32[]{:S(2)}, u32[]{:S(2)}) async-start(f32[64,4,512]{2,0,1:T(8,128)} %bitcast.196), calls=%async_computation.7 | async-start | bytes 1048576 | tf_op jit(solution)/shard_map/all_to_all | solution.py:268
  (24 other events, 49.3 us)
Sparse Core Ops, SparseCore 0:
  13.0 127.8 all-gather.5
  153.3 29.3 reduce-scatter.6
  610.1 12.5 all-gather.11
  753.9 23.8 reduce-scatter.10
  780.2 31.1 reduce-scatter.14
  814.9 251.4 reduce-scatter.16
Sparse Core Ops, SparseCore 1:
  157.1 113.9 all-gather.9
  274.4 131.9 all-gather.7
  458.0 148.8 reduce-scatter.12
  610.5 143.2 reduce-scatter.8

commit v2 on v1

--- a/solution.py
+++ b/solution.py
@@ -1,9 +1,8 @@
-from functools import partial
-
 import jax
 import jax.numpy as jnp
 from jax import lax
 from jax.sharding import PartitionSpec as P
+
 
 HEAD_DIM = 128
 EPSILON = 1e-06
@@ -34,15 +33,47 @@
     return lax.all_gather(value, ALL, axis=0, tiled=True)
 
 
-def scatter_all(value):
-    return lax.psum_scatter(value, ALL, scatter_dimension=0, tiled=True)
+def swap(value, axis, bit):
+    count = lax.axis_size(axis)
+    pairs = [(source, source ^ (1 << bit)) for source in range(count)]
+    return lax.ppermute(value, axis, pairs)
+
+
+def bits_of(axis):
+    return [(axis, bit) for bit in range(lax.axis_size(axis).bit_length() - 1)]
+
+
+def link_orders():
+    tensor_bits = bits_of("tensor")
+    dp_bits = bits_of("dp")
+    first, rest = tensor_bits[:1], tensor_bits[1:]
+    return (first + rest + dp_bits, first + dp_bits + rest)
+
+
+def halving(value, order):
+    dims = bits_of("dp")[::-1] + bits_of("tensor")[::-1]
+    width = value.shape[-1]
+    value = value.reshape((2,) * len(dims) + (-1, width))
+    for axis, bit in order:
+        dim = dims.index((axis, bit))
+        mine = (lax.axis_index(axis) >> bit) & 1
+        kept = lax.dynamic_index_in_dim(value, mine, dim)
+        sent = lax.dynamic_index_in_dim(value, 1 - mine, dim)
+        value = (kept.astype(F32) + swap(sent, axis, bit).astype(F32)).astype(BF16)
+    return value.reshape(-1, width)
+
+
+def scatter_all(parts):
+    return jnp.concatenate(
+        [halving(part, order) for part, order in zip(parts, link_orders())], axis=1
+    )
 
 
 def exchange_dp(value):
     return lax.all_to_all(value, "dp", 0, 0, tiled=False)
 
 
-def per_device(
+def layer(
     tokens,
     cotangent,
     routes,
@@ -87,7 +118,8 @@
         dense = dense + jnp.where(hit, gates[..., rank, None].astype(F32), 0.0)
     dense = dense.reshape(rows, LANES).astype(BF16)
     cot = jnp.where(valid, cotangent.reshape(rows, width), 0).astype(BF16)
-    cot_packed = gather_all(own_rows(jnp.concatenate([cot, dense], axis=1)))
+    cot_own = own_rows(jnp.concatenate([cot, dense], axis=1))
+    cot_packed = gather_all(cot_own)
 
     small = jnp.concatenate(
         [norm1_gain, norm2_gain, shared_switch, q_bias.reshape(-1), v_bias.reshape(-1)]
@@ -128,7 +160,8 @@
         expert_up.astype(BF16).transpose(0, 2, 1).reshape(-1, slice_d), shared_up.astype(BF16).T
     )
     down_sent = by_unit(expert_down.reshape(-1, slice_d), shared_down)
-    arrived = exchange_dp(jnp.stack([gate_sent, up_sent, down_sent], axis=1))
+    units_sent = jnp.stack([gate_sent, up_sent, down_sent], axis=1)
+    arrived = exchange_dp(units_sent)
     units = arrived.shape[2]
     routed = experts * expert_cols // n_dp
     arrived = arrived.transpose(1, 2, 0, 3).reshape(3, units, width)
@@ -176,9 +209,10 @@
     silu = gate_act * logistic
     inner = (silu * up_act).astype(BF16).astype(F32)
     inner_share = (inner * share).astype(BF16)
-    mixed = nn(inner_share, down_units).astype(BF16)
-    mixed = lax.psum_scatter(mixed, "dp", scatter_dimension=0, tiled=True)
-    mixed = lax.psum_scatter(mixed, "tensor", scatter_dimension=1, tiled=True)
+    half = width // 2
+    mixed = scatter_all(
+        [nn(inner_share, down_units[:, cut : cut + half]).astype(BF16) for cut in (0, half)]
+    )
 
     grad_inner_raw = nt(cot_all, down_units)
     grad_logit = (
@@ -190,16 +224,26 @@
     slope = logistic * (1.0 + gate_act * (1.0 - logistic))
     grad_gate_act = (grad_inner * up_act * slope).astype(BF16)
     grad_up_act = (grad_inner * silu).astype(BF16)
-    back_two = nn(grad_gate_act, gate_units) + nn(grad_up_act, up_units)
-    back_two = (back_two + grad_logit * switch.astype(F32)).astype(BF16)
-    back_two = scatter_all(back_two).astype(F32)
+    both_acts = jnp.concatenate([grad_gate_act, grad_up_act], axis=1)
+    both_units = jnp.concatenate([gate_units, up_units], axis=0)
+    back_parts = [
+        (
+            nn(both_acts, both_units[:, cut : cut + half])
+            + grad_logit * switch[:, cut : cut + half].astype(F32)
+        ).astype(BF16)
+        for cut in (0, half)
+    ]
     grad_down = tn(inner_share, cot_all)
     grad_gate = tn(grad_gate_act, normed_two)
     grad_up = tn(grad_up_act, normed_two)
     grad_switch = jnp.sum(grad_logit * normed_two.astype(F32), axis=0)
     sent_back = jnp.stack([grad_gate, grad_up, grad_down]).astype(BF16)
     sent_back = sent_back.reshape(3, units, n_dp, slice_d).transpose(2, 0, 1, 3)
-    returned = exchange_dp(sent_back).astype(F32)
+    sent_back, *back_parts = lax.optimization_barrier((sent_back, *back_parts))
+    returned = exchange_dp(sent_back)
+    returned = returned.astype(F32)
+    back_two = scatter_all(back_parts)
+    back_two = back_two.astype(F32)
 
     def split_units(value):
         routed_part = value[:, :routed].reshape(experts, expert_cols, slice_d)
@@ -209,7 +253,7 @@
     grad_up_experts, grad_up_shared = split_units(returned[:, 1])
     grad_down_experts, grad_down_shared = split_units(returned[:, 2])
 
-    unused_two, norm_two_back = jax.vjp(normalize, middle, gain_two)
+    _, norm_two_back = jax.vjp(normalize, middle, gain_two)
     grad_middle_norm, grad_gain_two = norm_two_back(back_two)
     grad_middle = own_rows(cot).astype(F32) + grad_middle_norm
     grad_attn = lax.all_gather(grad_middle.astype(BF16), "tensor", axis=0, tiled=True)
@@ -241,7 +285,7 @@
     ).astype(F32)
     back_one = nt(grad_qkv, weight_qkv)
     back_one = lax.psum_scatter(back_one, "tensor", scatter_dimension=0, tiled=True)
-    unused_one, norm_one_back = jax.vjp(normalize, inputs_own, gain_one)
+    _, norm_one_back = jax.vjp(normalize, inputs_own, gain_one)
     grad_input_norm, grad_gain_one = norm_one_back(back_one)
     grad_input = grad_middle + grad_input_norm
 
@@ -268,7 +312,7 @@
         return lax.all_to_all(value, "tensor", 1, 0, tiled=True)
 
     out_shape = (seqs, span, width // n_tensor)
-    output = jnp.where(valid, to_columns(middle) + mixed.astype(F32), 0.0).reshape(out_shape)
+    output = jnp.where(valid, to_columns(middle + mixed.astype(F32)), 0.0).reshape(out_shape)
     tokens_grad = jnp.where(valid, to_columns(grad_input), 0.0).reshape(out_shape)
     return (
         output,
@@ -318,6 +362,4 @@
 
 
 def solution(mesh):
-    return jax.shard_map(
-        per_device, mesh=mesh, in_specs=IN_SPECS, out_specs=OUT_SPECS, check_vma=False
-    )
+    return jax.shard_map(layer, mesh=mesh, in_specs=IN_SPECS, out_specs=OUT_SPECS, check_vma=False)

time: 1110 us -> 908 us (0.82)
  waiting for transfers between devices: 770 us -> 519 us
  starting transfers between devices: 18.5 us -> 54.1 us
  other arithmetic: 47.6 us -> 73.8 us
  matrix products: 111 us -> 97.9 us
    reduce_scatter x6 -> x3, waiting for transfers between devices: 309 us -> 25.3 us  [the longest x1 25.3 us: layer(): lax.psum_scatter(attn_part, 'tensor', scatter_dimension=0, tiled=True)]
    ppermute x0 -> x20, waiting for transfers between devices: none -> 207 us  [swap(): return lax.ppermute(value, axis, pairs)]
    all_to_all x2, waiting for transfers between devices: 325 us -> 145 us  [exchange_dp(): return lax.all_to_all(value, 'dp', 0, 0, tiled=False)]
    ppermute x0 -> x20, starting transfers between devices: none -> 35.1 us  [swap(): return lax.ppermute(value, axis, pairs)]
    convert_element_type x12 -> x27, other arithmetic: 9.4 us -> 35.9 us  [the longest x16 16.6 us: halving(): value = (kept.astype(F32) + swap(sent, axis, bit).astype(F32)).astype(BF16)]
    all_gather x2, waiting for transfers between devices: 91.7 us -> 106 us  [the longest x1 90.8 us: layer(): attn_weights = lax.all_gather(attn_weights, 'dp', axis=0, tiled=True)]
    dot_general x6 -> x7, matrix products: 40.1 us -> 31.2 us  [nn(): lax.dot_general(left, right, (((1,), (0,)), ((), ())), preferred_element_...]
    unnamed x107 -> x129, local copies, waits for them, and re-layouts: 35 us -> 29.6 us
  transfers between devices with their start and end apart: 14 -> 31, of which waited for: 7 -> 21; matrix products, arithmetic and copies ran while one was open for 13% -> 14% of each run, Pallas kernels for 0% -> 0%
where the time goes in v2:
time: 908 us; the launch traced here: 900 us
  waiting for transfers between devices  519 us (57%)
  matrix products  97.9 us (11%)
  other arithmetic  73.8 us (8%)
  blocking collectives  73.7 us (8%)
  local copies, waits for them, and re-layouts  64 us (7%)
  starting transfers between devices  54.1 us (6%)
  between operations  17.1 us (2%)
    ppermute x20, waiting for transfers between devices, swap(): return lax.ppermute(value, axis, pairs)  207 us
    all_to_all x2, waiting for transfers between devices, exchange_dp(): return lax.all_to_all(value, 'dp', 0, 0, tiled=False)  145 us
    all_gather x1, waiting for transfers between devices, layer(): attn_weights = lax.all_gather(attn_weights, 'dp', axis=0, tiled=True)  90.8 us
    psum x1, blocking collectives, layer(): pack = lax.psum(pack, ALL)  40.2 us
    dot_general x6, matrix products, nt(): lax.dot_general(left, right, (((1,), (1,)), ((), ())), preferred_element_...  39.6 us
    all_gather x2, waiting for transfers between devices, gather_all(): return lax.all_gather(value, ALL, axis=0, tiled=True)  35.6 us
    ppermute x20, starting transfers between devices, swap(): return lax.ppermute(value, axis, pairs)  35.1 us
    all_gather x1, blocking collectives, layer(): small = lax.all_gather(small[None, :], 'dp', axis=0, tiled=True)  33.5 us
  transfers between devices with their start and end apart: 31, of which 21 were waited for; matrix products, arithmetic and copies ran while one was open for 14% of the time, Pallas kernels for 0%

profile of v2, /device:TPU:0, one launch (start us, length us, event | category | flops | bytes accessed | tf_op | source)
XLA Modules:
  0.0 899.6 jit_solution(8376816481608443545)
XLA Ops:
  13.3 33.5 %all-gather = bf16[8,1,896]{2,1,0:T(2,128)(2,1)S(1)} all-gather(bf16[1,1,896]{2,1,0:T(2,128)(2,1)S(1)} %bitcast.271), channel_id=1, replica_groups=mesh['dp'=8,'tensor'=4] {'dp'}, dimensions={0}, use_global_device_ids=true | all-gather | bytes 16128 | tf_op jit(solution)/shard_map/all_gather | solution.py:127
  50.1 90.8 %all-gather.6.cloned.1.call-done = bf16[2048,2048]{0,1:T(8,128)(2,1)} async-done(((bf16[256,2048]{0,1:T(8,128)(2,1)}), bf16[2048,2048]{0,1:T(8,128)(2,1)}) %all-gather.6.cloned.1.call-update) | async-done | bytes 8388624 | tf_op jit(solution)/shard_map/all_gather | solution.py:143
  140.9 4.9 fusion.7
  160.2 25.3 %reduce-scatter.4.cloned.1.call-done = f32[64,2048]{1,0:T(8,128)} async-done(((f32[256,2048]{1,0:T(8,128)}), f32[64,2048]{1,0:T(8,128)}) %reduce-scatter.4.cloned.1.call-update) | async-done | bytes 524304 | tf_op jit(solution)/shard_map/reduce_scatter | solution.py:193
  204.3 5.5 all-to-all-start
  210.1 144.8 %all-to-all-done = bf16[8,3,440,256]{3,2,1,0:T(8,128)(2,1)} async-done(((bf16[8,3,440,256]{3,2,1,0:T(8,128)(2,1)}), bf16[8,3,440,256]{3,2,1,0:T(8,128)(2,1)}, u32[]{:S(2)}, u32[]{:S(2)}) %all-to-all-start) | async-done | bytes 5406752 | tf_op jit(solution)/shard_map/all_to_all | solution.py:73
  365.7 8.2 fusion.3
  373.9 35.6 %all-gather.8.cloned.1.call-done = bf16[2048,2048]{1,0:T(8,128)(2,1)} async-done(((bf16[64,2048]{1,0:T(8,128)(2,1)}), bf16[2048,2048]{1,0:T(8,128)(2,1)}) %all-gather.8.cloned.1.call-update) | async-done | bytes 8388624 | tf_op jit(solution)/shard_map/all_gather | solution.py:33
  409.5 5.8 fusion.83
  415.8 5.7 fusion.82
  421.7 9.9 %multiply_convert_fusion.1 = (bf16[2048,440]{0,1:T(8,128)(2,1)}, bf16[2048,440]{0,1:T(8,128)(2,1)}, bf16[2048,440]{0,1:T(8,128)(2,1)S(1)}, f32[2048,440]{0,1:T(8,128)}) fusion(f32[2048,440]{0,1:T(8,128)} %fusion.82, f32[2048,440]{0,1:T(8,128)S(1)} %copy-done.34, f32[2048,176]{0,1:T(8,128)S(1)} %broadcast_in_dim.165, f32[2048,264]{0,1:T(8,128)S(1)} %copy-done.23, ...), kind=kOutput, calls=%fused_computation.32 | convolution fusion | flops 3709009920 | bytes 30015488 | tf_op jit(solution)/shard_map/dot_general | solution.py:21
  431.7 7.9 fusion.13
  454.7 6.5 add_convert_fusion.1
  461.3 7.7 add_convert_fusion
  488.8 18.6 %collective-permute-done.16 = bf16[2,2,1,2,1,64,1024]{6,5,4,3,2,1,0:T(8,128)(2,1)} collective-permute-done((bf16[2,2,1,2,1,64,1024]{6,5,4,3,2,1,0:T(8,128)(2,1)}, bf16[2,2,1,2,1,64,1024]{6,5,4,3,2,1,0:T(8,128)(2,1)}, u32[]{:S(2)}, u32[]{:S(2)}) %collective-permute-start.16) | collective-permute-done | bytes 1048608 | tf_op jit(solution)/shard_map/ppermute | solution.py:39
  516.6 5.8 collective-permute-done.17
  531.0 6.2 collective-permute-done.18
  542.3 4.8 collective-permute-done.14
  549.3 15.4 %all-gather.12.cloned.1.call-done = bf16[256,2048]{1,0:T(8,128)(2,1)} async-done(((bf16[64,2048]{1,0:T(8,128)(2,1)}), bf16[256,2048]{1,0:T(8,128)(2,1)}) %all-gather.12.cloned.1.call-update) | async-done | bytes 1048592 | tf_op jit(solution)/shard_map/all_gather | solution.py:259
  571.2 6.2 fusion.5
  580.5 4.5 convolution_convert_fusion
  585.0 8.0 pad_maximum_fusion
  593.0 6.0 all-to-all-start.3
  615.8 64.8 %collective-permute-done.6 = bf16[2,2,1,2,1,64,1024]{6,5,4,3,2,1,0:T(8,128)(2,1)} collective-permute-done((bf16[2,2,1,2,1,64,1024]{6,5,4,3,2,1,0:T(8,128)(2,1)}, bf16[2,2,1,2,1,64,1024]{6,5,4,3,2,1,0:T(8,128)(2,1)}, u32[]{:S(2)}, u32[]{:S(2)}) %collective-permute-start.6) | collective-permute-done | bytes 1048608 | tf_op jit(solution)/shard_map/ppermute | solution.py:39
  687.6 5.1 multiply_reduce_fusion
  692.7 59.4 %collective-permute-done.7 = bf16[2,1,1,2,1,64,1024]{6,5,4,3,2,1,0:T(8,128)(2,1)S(1)} collective-permute-done((bf16[2,1,1,2,1,64,1024]{6,5,4,3,2,1,0:T(8,128)(2,1)S(1)}, bf16[2,1,1,2,1,64,1024]{6,5,4,3,2,1,0:T(8,128)(2,1)S(1)}, u32[]{:S(2)}, u32[]{:S(2)}) %collective-permute-start.7) | collective-permute-done | bytes 524320 | tf_op jit(solution)/shard_map/ppermute | solution.py:39
  752.4 17.7 %collective-permute-start.8 = (bf16[1,1,1,2,1,64,1024]{6,5,4,3,2,1,0:T(8,128)(2,1)S(1)}, bf16[1,1,1,2,1,64,1024]{6,5,4,3,2,1,0:T(8,128)(2,1)S(1)}, u32[]{:S(2)}, u32[]{:S(2)}) collective-permute-start(bf16[1,1,1,2,1,64,1024]{6,5,4,3,2,1,0:T(8,128)(2,1)S(1)} %constant_dynamic-slice_fusion.14), channel_id=1, source_target_pairs={{0,16},{4,20},{8,24},{12,28},{16,0},{20,4},{24,8},{28,12},{1,17},{... | collective-permute-start | bytes 786440 | tf_op jit(solution)/shard_map/ppermute | solution.py:39
  770.4 26.7 %collective-permute-done.8 = bf16[1,1,1,2,1,64,1024]{6,5,4,3,2,1,0:T(8,128)(2,1)S(1)} collective-permute-done((bf16[1,1,1,2,1,64,1024]{6,5,4,3,2,1,0:T(8,128)(2,1)S(1)}, bf16[1,1,1,2,1,64,1024]{6,5,4,3,2,1,0:T(8,128)(2,1)S(1)}, u32[]{:S(2)}, u32[]{:S(2)}) %collective-permute-start.8) | collective-permute-done | bytes 262176 | tf_op jit(solution)/shard_map/ppermute | solution.py:39
  802.3 4.4 collective-permute-done.4
  807.0 8.1 copy_convert_fusion
  823.1 5.1 slice_bitcast_fusion
  844.1 40.2 %psum.7 = f32[8,1280]{1,0:T(8,128)S(1)} all-reduce(f32[8,1280]{1,0:T(8,128)S(1)} %pad_maximum_fusion.8), channel_id=1, replica_groups=mesh['dp'=8,'tensor'=4] {'dp','tensor'}, use_global_device_ids=true, to_apply=%region_16.17 | all-reduce | flops 10240 | bytes 81920 | tf_op jit(solution)/shard_map/psum | solution.py:305
  (337 shorter events, 183.2 us)
Async XLA Ops:
  8.0 132.9 %all-gather.6.cloned.1.call-start = ((), (), s32[]{:S(2)}) async-start(), calls=%async_computation.7 | async-start | bytes 9437184 | tf_op jit(solution)/shard_map/all_gather | solution.py:143
  12.8 172.7 %reduce-scatter.4.cloned.1.call-start = ((), (), s32[]{:S(2)}) async-start(), calls=%async_computation.8 | async-start | bytes 2621440 | tf_op jit(solution)/shard_map/reduce_scatter | solution.py:193
  50.1 135.4 %copy-start.9 = (f32[2,128,2048]{2,1,0:T(8,128)}, f32[2,128,2048]{2,1,0:T(8,128)S(1)}, u32[]{:S(2)}) copy-start(f32[2,128,2048]{2,1,0:T(8,128)S(1)} %get-tuple-element.100) | copy-start | bytes 6291460
  156.0 206.7 %all-gather.10.cloned.1.call-start = ((), (), s32[]{:S(2)}) async-start(), calls=%async_computation.10 | async-start | bytes 9191424 | tf_op jit(solution)/shard_map/all_gather | solution.py:33
  160.1 249.4 %all-gather.8.cloned.1.call-start = ((), (), s32[]{:S(2)}) async-start(), calls=%async_computation.9 | async-start | bytes 8650752 | tf_op jit(solution)/shard_map/all_gather | solution.py:33
  204.3 150.6 %all-to-all-start = ((bf16[8,3,440,256]{3,2,1,0:T(8,128)(2,1)}), bf16[8,3,440,256]{3,2,1,0:T(8,128)(2,1)}, u32[]{:S(2)}, u32[]{:S(2)}) async-start(bf16[8,3,440,256]{3,2,1,0:T(8,128)(2,1)} %pad_maximum_fusion.1), calls=%async_computation.1 | async-start | bytes 10813440 | tf_op jit(solution)/shard_map/all_to_all | solution.py:73
  209.8 354.9 %all-gather.12.cloned.1.call-start = ((), (), s32[]{:S(2)}) async-start(), calls=%async_computation.11 | async-start | bytes 1310720 | tf_op jit(solution)/shard_map/all_gather | solution.py:259
  472.9 4.4 collective-permute-start.15
  474.7 8.5 collective-permute-start.10
  481.8 25.6 %collective-permute-start.16 = (bf16[2,2,1,2,1,64,1024]{6,5,4,3,2,1,0:T(8,128)(2,1)}, bf16[2,2,1,2,1,64,1024]{6,5,4,3,2,1,0:T(8,128)(2,1)}, u32[]{:S(2)}, u32[]{:S(2)}) collective-permute-start(bf16[2,2,1,2,1,64,1024]{6,5,4,3,2,1,0:T(8,128)(2,1)} %constant_dynamic-slice_fusion.6), channel_id=1, source_target_pairs={{0,4},{4,0},{8,12},{12,8},{16,20},{20,16},{24,28},{28,24},{1,5},{5... | collective-permute-start | bytes 3145736 | tf_op jit(solution)/shard_map/ppermute | solution.py:39
  488.2 25.4 %collective-permute-start.11 = (bf16[2,2,2,1,1,64,1024]{6,5,4,3,2,1,0:T(8,128)(2,1)}, bf16[2,2,2,1,1,64,1024]{6,5,4,3,2,1,0:T(8,128)(2,1)}, u32[]{:S(2)}, u32[]{:S(2)}) collective-permute-start(bf16[2,2,2,1,1,64,1024]{6,5,4,3,2,1,0:T(8,128)(2,1)} %constant_dynamic-slice_fusion.11), channel_id=1, source_target_pairs={{0,2},{1,3},{2,0},{3,1},{4,6},{5,7},{6,4},{7,5},{8,10},{9,11},{10,... | collective-permute-start | bytes 3145736 | tf_op jit(solution)/shard_map/ppermute | solution.py:39
  509.1 13.3 %collective-permute-start.17 = (bf16[2,1,1,2,1,64,1024]{6,5,4,3,2,1,0:T(8,128)(2,1)S(1)}, bf16[2,1,1,2,1,64,1024]{6,5,4,3,2,1,0:T(8,128)(2,1)S(1)}, u32[]{:S(2)}, u32[]{:S(2)}) collective-permute-start(bf16[2,1,1,2,1,64,1024]{6,5,4,3,2,1,0:T(8,128)(2,1)S(1)} %constant_dynamic-slice_fusion.5), channel_id=1, source_target_pairs={{0,8},{4,12},{8,0},{12,4},{16,24},{20,28},{24,16},{28,20},{1,9},{5... | collective-permute-start | bytes 1572872 | tf_op jit(solution)/shard_map/ppermute | solution.py:39
  516.0 13.2 %collective-permute-start.12 = (bf16[2,2,1,1,1,64,1024]{6,5,4,3,2,1,0:T(8,128)(2,1)}, bf16[2,2,1,1,1,64,1024]{6,5,4,3,2,1,0:T(8,128)(2,1)S(1)}, u32[]{:S(2)}, u32[]{:S(2)}) collective-permute-start(bf16[2,2,1,1,1,64,1024]{6,5,4,3,2,1,0:T(8,128)(2,1)} %constant_dynamic-slice_fusion.10), channel_id=1, source_target_pairs={{0,4},{4,0},{8,12},{12,8},{16,20},{20,16},{24,28},{28,24},{1,5},{5... | collective-permute-start | bytes 1572872 | tf_op jit(solution)/shard_map/ppermute | solution.py:39
  523.7 13.4 %collective-permute-start.18 = (bf16[1,1,1,2,1,64,1024]{6,5,4,3,2,1,0:T(8,128)(2,1)S(1)}, bf16[1,1,1,2,1,64,1024]{6,5,4,3,2,1,0:T(8,128)(2,1)S(1)}, u32[]{:S(2)}, u32[]{:S(2)}) collective-permute-start(bf16[1,1,1,2,1,64,1024]{6,5,4,3,2,1,0:T(8,128)(2,1)S(1)} %constant_dynamic-slice_fusion.4), channel_id=1, source_target_pairs={{0,16},{4,20},{8,24},{12,28},{16,0},{20,4},{24,8},{28,12},{1,17},{... | collective-permute-start | bytes 786440 | tf_op jit(solution)/shard_map/ppermute | solution.py:39
  529.4 11.1 %collective-permute-start.13 = (bf16[2,1,1,1,1,64,1024]{6,5,4,3,2,1,0:T(8,128)(2,1)S(1)}, bf16[2,1,1,1,1,64,1024]{6,5,4,3,2,1,0:T(8,128)(2,1)S(1)}, u32[]{:S(2)}, u32[]{:S(2)}) collective-permute-start(bf16[2,1,1,1,1,64,1024]{6,5,4,3,2,1,0:T(8,128)(2,1)S(1)} %constant_dynamic-slice_fusion.9), channel_id=1, source_target_pairs={{0,8},{4,12},{8,0},{12,4},{16,24},{20,28},{24,16},{28,20},{1,9},{5... | collective-permute-start | bytes 786440 | tf_op jit(solution)/shard_map/ppermute | solution.py:39
  537.3 5.0 collective-permute-start.19
  540.7 6.5 collective-permute-start.14
  549.3 265.9 %reduce-scatter.6.cloned.1.call-start = ((), (), s32[]{:S(2)}) async-start(), calls=%async_computation.12 | async-start | bytes 2621440 | tf_op jit(solution)/shard_map/reduce_scatter | solution.py:287
  577.4 309.4 %reduce-scatter.8.cloned.1.call-start = ((), (), s32[]{:S(2)}) async-start(), calls=%async_computation.13 | async-start | bytes 9437184 | tf_op jit(solution)/shard_map/reduce_scatter | solution.py:283
  593.0 214.0 %all-to-all-start.3 = ((bf16[8,3,440,256]{3,2,1,0:T(8,128)(2,1)}), bf16[8,3,440,256]{3,2,1,0:T(8,128)(2,1)}, u32[]{:S(2)}, u32[]{:S(2)}) async-start(bf16[8,3,440,256]{3,2,1,0:T(8,128)(2,1)} %maximum_bitcast_fusion), calls=%async_computation.6 | async-start | bytes 10813440 | tf_op jit(solution)/shard_map/all_to_all | solution.py:73
  603.2 4.2 collective-permute-start.5
  607.1 4.4 collective-permute-start
  609.5 71.0 %collective-permute-start.6 = (bf16[2,2,1,2,1,64,1024]{6,5,4,3,2,1,0:T(8,128)(2,1)}, bf16[2,2,1,2,1,64,1024]{6,5,4,3,2,1,0:T(8,128)(2,1)}, u32[]{:S(2)}, u32[]{:S(2)}) collective-permute-start(bf16[2,2,1,2,1,64,1024]{6,5,4,3,2,1,0:T(8,128)(2,1)} %constant_dynamic-slice_fusion.16), channel_id=1, source_target_pairs={{0,4},{4,0},{8,12},{12,8},{16,20},{20,16},{24,28},{28,24},{1,5},{5... | collective-permute-start | bytes 3145736 | tf_op jit(solution)/shard_map/ppermute | solution.py:39
  615.0 68.4 %collective-permute-start.1 = (bf16[2,2,2,1,1,64,1024]{6,5,4,3,2,1,0:T(8,128)(2,1)}, bf16[2,2,2,1,1,64,1024]{6,5,4,3,2,1,0:T(8,128)(2,1)}, u32[]{:S(2)}, u32[]{:S(2)}) collective-permute-start(bf16[2,2,2,1,1,64,1024]{6,5,4,3,2,1,0:T(8,128)(2,1)} %constant_dynamic-slice_fusion.21), channel_id=1, source_target_pairs={{0,2},{1,3},{2,0},{3,1},{4,6},{5,7},{6,4},{7,5},{8,10},{9,11},{10,... | collective-permute-start | bytes 3145736 | tf_op jit(solution)/shard_map/ppermute | solution.py:39
  682.2 69.9 %collective-permute-start.7 = (bf16[2,1,1,2,1,64,1024]{6,5,4,3,2,1,0:T(8,128)(2,1)S(1)}, bf16[2,1,1,2,1,64,1024]{6,5,4,3,2,1,0:T(8,128)(2,1)S(1)}, u32[]{:S(2)}, u32[]{:S(2)}) collective-permute-start(bf16[2,1,1,2,1,64,1024]{6,5,4,3,2,1,0:T(8,128)(2,1)S(1)} %constant_dynamic-slice_fusion.15), channel_id=1, source_target_pairs={{0,8},{4,12},{8,0},{12,4},{16,24},{20,28},{24,16},{28,20},{1,9},{5... | collective-permute-start | bytes 1572872 | tf_op jit(solution)/shard_map/ppermute | solution.py:39
  685.1 85.0 %collective-permute-start.2 = (bf16[2,2,1,1,1,64,1024]{6,5,4,3,2,1,0:T(8,128)(2,1)S(1)}, bf16[2,2,1,1,1,64,1024]{6,5,4,3,2,1,0:T(8,128)(2,1)S(1)}, u32[]{:S(2)}, u32[]{:S(2)}) collective-permute-start(bf16[2,2,1,1,1,64,1024]{6,5,4,3,2,1,0:T(8,128)(2,1)S(1)} %constant_dynamic-slice_fusion.20), channel_id=1, source_target_pairs={{0,4},{4,0},{8,12},{12,8},{16,20},{20,16},{24,28},{28,24},{1,5},{5... | collective-permute-start | bytes 1572872 | tf_op jit(solution)/shard_map/ppermute | solution.py:39
  752.4 44.8 %collective-permute-start.8 = (bf16[1,1,1,2,1,64,1024]{6,5,4,3,2,1,0:T(8,128)(2,1)S(1)}, bf16[1,1,1,2,1,64,1024]{6,5,4,3,2,1,0:T(8,128)(2,1)S(1)}, u32[]{:S(2)}, u32[]{:S(2)}) collective-permute-start(bf16[1,1,1,2,1,64,1024]{6,5,4,3,2,1,0:T(8,128)(2,1)S(1)} %constant_dynamic-slice_fusion.14), channel_id=1, source_target_pairs={{0,16},{4,20},{8,24},{12,28},{16,0},{20,4},{24,8},{28,12},{1,17},{... | collective-permute-start | bytes 786440 | tf_op jit(solution)/shard_map/ppermute | solution.py:39
  770.3 29.3 %collective-permute-start.3 = (bf16[2,1,1,1,1,64,1024]{6,5,4,3,2,1,0:T(8,128)(2,1)S(1)}, bf16[2,1,1,1,1,64,1024]{6,5,4,3,2,1,0:T(8,128)(2,1)S(1)}, u32[]{:S(2)}, u32[]{:S(2)}) collective-permute-start(bf16[2,1,1,1,1,64,1024]{6,5,4,3,2,1,0:T(8,128)(2,1)S(1)} %constant_dynamic-slice_fusion.19), channel_id=1, source_target_pairs={{0,8},{4,12},{8,0},{12,4},{16,24},{20,28},{24,16},{28,20},{1,9},{5... | collective-permute-start | bytes 786440 | tf_op jit(solution)/shard_map/ppermute | solution.py:39
  797.3 5.0 collective-permute-start.9
  799.8 6.9 collective-permute-start.4
  819.6 21.0 %all-to-all-start.2 = ((f32[64,4,512]{2,0,1:T(8,128)}), f32[64,4,512]{2,0,1:T(8,128)S(1)}, u32[]{:S(2)}, u32[]{:S(2)}) async-start(f32[64,4,512]{2,0,1:T(8,128)} %bitcast.202), calls=%async_computation.4 | async-start | bytes 1048576 | tf_op jit(solution)/shard_map/all_to_all | solution.py:312
  840.6 45.1 %all-to-all-start.1 = ((f32[64,4,512]{2,0,1:T(8,128)}), f32[64,4,512]{2,0,1:T(8,128)S(1)}, u32[]{:S(2)}, u32[]{:S(2)}) async-start(f32[64,4,512]{2,0,1:T(8,128)} %bitcast.203), calls=%async_computation.2 | async-start | bytes 1048576 | tf_op jit(solution)/shard_map/all_to_all | solution.py:312
  (52 other events, 383.6 us)
Sparse Core Ops, SparseCore 0:
  13.0 127.8 all-gather.5
  156.1 29.3 reduce-scatter.3
  549.4 15.2 all-gather.11
  577.5 31.1 reduce-scatter.5
  612.2 241.2 reduce-scatter.7
Sparse Core Ops, SparseCore 1:
  160.2 114.1 all-gather.9
  277.7 131.7 all-gather.7
